TPU v7x, 8 devices: a whole 2x2x1 slice. The times are simulated.
8 devices in a mesh: emb: 8 (over z, y, x, core).
Axes of the slice: x: 2, y: 2, z: 1, core: 2. Of those that a mesh axis runs over, the one named last changes fastest.
Arguments:
- tok_ids: int32 [8192], P('emb')
- x_in: bfloat16 [8192, 768], P('emb')
- d_out: bfloat16 [8192, 768], P('emb')
- ple_tables: bfloat16 [5, 50304, 768], P(None, 'emb')
- w_up: bfloat16 [5, 768, 3072], replicated
- w_down: bfloat16 [5, 3072, 768], replicated
- w_gate: bfloat16 [5, 768, 768], replicated
- w_proj: bfloat16 [5, 768, 768], replicated
Outputs:
- output 1: bfloat16 [8192, 768], P('emb')
- output 2: float32 [5, 50304, 768], P(None, 'emb')
- output 3: float32 [5, 768, 3072], replicated
- output 4: float32 [5, 3072, 768], replicated
- output 5: float32 [5, 768, 768], replicated
- output 6: float32 [5, 768, 768], replicated
All inputs are finite; a program needn't handle non-finite values.
Results may differ from a plain program's by a relative error of at most 0.0177945.
Values are sent between devices in bfloat16 or wider.
A program may use at most 1.25 GiB of HBM per device.

v0:
```python
import jax
import jax.numpy as jnp
from jax import lax
from jax.sharding import PartitionSpec as P

EPS = 1e-6
CAP_DIV = 4


def gelu_tanh(pre_act):
    return jax.nn.gelu(pre_act, approximate=True)


def gelu_back(pre_act, grad_out):
    _, pull_back = jax.vjp(gelu_tanh, pre_act.astype(jnp.float32))
    return pull_back(grad_out.astype(jnp.float32))[0]


def layer_fwd(x_cur, up_mat, down_mat, gate_mat, proj_mat, emb_rows):
    x_wide = x_cur.astype(jnp.float32)
    inv_rms = lax.rsqrt(jnp.mean(x_wide * x_wide, axis=-1, keepdims=True) + EPS)
    normed = (x_wide * inv_rms).astype(jnp.bfloat16)
    hidden = jnp.dot(normed, up_mat, preferred_element_type=jnp.float32).astype(jnp.bfloat16)
    act_out = gelu_tanh(hidden.astype(jnp.float32)).astype(jnp.bfloat16)
    mlp_out = jnp.dot(act_out, down_mat, preferred_element_type=jnp.float32).astype(jnp.bfloat16)
    gate_pre = jnp.dot(normed, gate_mat, preferred_element_type=jnp.float32).astype(jnp.bfloat16)
    gate_act = gelu_tanh(gate_pre.astype(jnp.float32)).astype(jnp.bfloat16)
    mix_rows = (gate_act.astype(jnp.float32) * emb_rows.astype(jnp.float32)).astype(jnp.bfloat16)
    ple_out = jnp.dot(mix_rows, proj_mat, preferred_element_type=jnp.float32).astype(jnp.bfloat16)
    x_next = (x_wide + mlp_out.astype(jnp.float32) + ple_out.astype(jnp.float32)).astype(jnp.bfloat16)
    return x_next, (x_wide, inv_rms, normed, hidden, act_out, gate_pre, gate_act, mix_rows)


def layer_bwd(d_x, saved, emb_rows, up_mat, down_mat, gate_mat, proj_mat):
    x_wide, inv_rms, normed, hidden, act_out, gate_pre, gate_act, mix_rows = saved
    g_out = d_x.astype(jnp.bfloat16)
    d_act = jnp.einsum("nd,fd->nf", g_out, down_mat, preferred_element_type=jnp.float32).astype(jnp.bfloat16)
    d_hidden = gelu_back(hidden, d_act).astype(jnp.bfloat16)
    d_mix = jnp.einsum("nd,ed->ne", g_out, proj_mat, preferred_element_type=jnp.float32).astype(jnp.bfloat16)
    d_rows = gate_act.astype(jnp.float32) * d_mix.astype(jnp.float32)
    d_gate_act = (emb_rows.astype(jnp.float32) * d_mix.astype(jnp.float32)).astype(jnp.bfloat16)
    d_gate_pre = gelu_back(gate_pre, d_gate_act).astype(jnp.bfloat16)
    d_norm = jnp.einsum("nf,df->nd", d_hidden, up_mat, preferred_element_type=jnp.float32) + jnp.einsum("ne,de->nd", d_gate_pre, gate_mat, preferred_element_type=jnp.float32)
    d_x_new = d_x + inv_rms * d_norm - inv_rms ** 3 * x_wide * jnp.mean(d_norm * x_wide, axis=-1, keepdims=True)
    g_up = jnp.einsum("nd,nf->df", normed, d_hidden, preferred_element_type=jnp.float32)
    g_down = jnp.einsum("nf,nd->fd", act_out, g_out, preferred_element_type=jnp.float32)
    g_gate = jnp.einsum("nd,ne->de", normed, d_gate_pre, preferred_element_type=jnp.float32)
    g_proj = jnp.einsum("ne,nd->ed", mix_rows, g_out, preferred_element_type=jnp.float32)
    return d_x_new, (g_up, g_down, g_gate, g_proj), d_rows


def solution(mesh):
    shards = mesh.shape["emb"]

    def device_step(tok_ids, x_in, d_out, ple_tables, w_up, w_down, w_gate, w_proj):
        layers = ple_tables.shape[0]
        rows_dev = ple_tables.shape[1]
        cap_rows = tok_ids.shape[0] // CAP_DIV
        owner_dev = tok_ids // rows_dev
        local_row = tok_ids - owner_dev * rows_dev
        owner_hot = (owner_dev[:, None] == jnp.arange(shards, dtype=jnp.int32)[None, :]).astype(jnp.int32)
        slot_rank = jnp.sum((jnp.cumsum(owner_hot, axis=0) - owner_hot) * owner_hot, axis=1)
        dest_slot = owner_dev * cap_rows + slot_rank
        req_send = jnp.zeros((shards * cap_rows,), jnp.int32).at[dest_slot].set(local_row)
        req_recv = lax.all_to_all(req_send, "emb", 0, 0, tiled=True)
        x_cur = x_in
        saved_list = []
        rows_list = []
        for layer_idx in range(layers):
            served = jnp.take(ple_tables[layer_idx], req_recv, axis=0)
            returned = lax.all_to_all(served, "emb", 0, 0, tiled=True)
            emb_rows = jnp.take(returned, dest_slot, axis=0)
            x_cur, saved = layer_fwd(x_cur, w_up[layer_idx], w_down[layer_idx], w_gate[layer_idx], w_proj[layer_idx], emb_rows)
            saved_list.append(saved)
            rows_list.append(emb_rows)
        d_x = d_out.astype(jnp.float32)
        grads_by_layer = [None] * layers
        tables_by_layer = [None] * layers
        for layer_idx in reversed(range(layers)):
            d_x, grads, d_rows = layer_bwd(d_x, saved_list[layer_idx], rows_list[layer_idx], w_up[layer_idx], w_down[layer_idx], w_gate[layer_idx], w_proj[layer_idx])
            grad_send = jnp.zeros((shards * cap_rows, d_rows.shape[1]), jnp.float32).at[dest_slot].set(d_rows)
            grad_recv = lax.all_to_all(grad_send, "emb", 0, 0, tiled=True)
            tables_by_layer[layer_idx] = jax.ops.segment_sum(grad_recv, req_recv, num_segments=rows_dev)
            grads_by_layer[layer_idx] = lax.psum(grads, "emb")
        grad_stacks = [jnp.stack([entry[grad_pos] for entry in grads_by_layer]) for grad_pos in range(4)]
        return (x_cur, jnp.stack(tables_by_layer), grad_stacks[0], grad_stacks[1], grad_stacks[2], grad_stacks[3])

    return jax.shard_map(
        device_step,
        mesh=mesh,
        in_specs=(P("emb"), P("emb", None), P("emb", None), P(None, "emb", None), P(), P(), P(), P()),
        out_specs=(P("emb", None), P(None, "emb", None), P(), P(), P(), P()),
        check_vma=False,
    )
```

profile of v0, /device:TPU:0, one launch (start us, length us, event | category | flops | bytes accessed | tf_op | source)
XLA Modules:
  0.0 2396.7 jit_solution(4233504072488339989)
XLA Ops:
  20.6 33.0 %slice_bitcast_fusion = (bf16[6288,768]{1,0:T(8,128)(2,1)}, bf16[6288,768]{1,0:T(8,128)(2,1)}, bf16[6288,768]{1,0:T(8,128)(2,1)}, bf16[6288,768]{1,0:T(8,128)(2,1)}, bf16[6288,768]{1,0:T(8,128)(2,1)}) fusion(bf16[5,6288,768]{2,1,0:T(8,128)(2,1)} %param.15), kind=kLoop, calls=%fused_computation.121 | loop fusion | bytes 96583680 | tf_op jit(solution)/shard_map/squeeze | solution.py:70
  58.9 9.5 convolution_convert_fusion.4
  74.0 13.4 gather_fusion.8
  87.5 15.0 gather_fusion.2
  102.5 15.2 gather_fusion.4
  117.8 15.0 gather_fusion.6
  132.8 15.0 gather_fusion
  147.8 9.2 broadcast_select_fusion
  160.0 10.8 fusion.229
  170.8 27.0 %all-to-all-done.1 = bf16[8,256,768]{2,1,0:T(8,128)(2,1)S(1)} async-done(((bf16[8,256,768]{2,1,0:T(8,128)(2,1)}), bf16[8,256,768]{2,1,0:T(8,128)(2,1)S(1)}, u32[]{:S(2)}, u32[]{:S(2)}) %all-to-all-start.1) | async-done | bytes 3145760 | tf_op jit(solution)/shard_map/all_to_all | solution.py:71
  202.1 7.9 gather_fusion.1
  220.2 9.4 convolution_convert_fusion.3
  229.6 10.2 all-to-all-done.2
  248.7 10.0 fusion.232
  267.9 9.4 convolution_convert_fusion.2
  283.8 7.9 gather_fusion.5
  291.7 10.0 fusion.235
  310.8 9.4 convolution_convert_fusion.1
  330.2 10.0 fusion.238
  345.0 17.5 all-to-all-done.5
  362.5 7.9 gather_fusion.9
  370.4 7.9 convolution_convert_fusion
  380.9 15.6 fusion.7
  396.6 8.7 fusion.75
  413.0 18.2 fusion.10
  437.7 9.4 fusion.81
  450.1 17.9 fusion.13
  474.6 9.6 fusion.87
  486.9 17.0 fusion.16
  510.5 9.2 fusion.93
  527.9 19.1 fusion.67
  547.0 10.3 convolution_bitcast_fusion.8
  557.4 10.3 convolution_bitcast_fusion.7
  567.8 7.7 convolution_bitcast_fusion.6
  575.5 7.4 convolution_bitcast_fusion.5
  583.0 11.1 convolution_bitcast_fusion.4
  594.1 11.4 convolution_bitcast_fusion.3
  605.6 10.9 convolution_bitcast_fusion.2
  616.4 13.2 convolution_bitcast_fusion.1
  629.7 10.3 convolution_bitcast_fusion
  676.6 9.8 scatter_custom_fusion.1
  690.2 9.7 scatter_custom_fusion.3
  699.8 117.4 %all-to-all-done.6 = f32[8,256,768]{2,1,0:T(8,128)} async-done(((f32[8,256,768]{2,1,0:T(8,128)}), f32[8,256,768]{2,1,0:T(8,128)}, u32[]{:S(2)}, u32[]{:S(2)}) %all-to-all-start.6) | async-done | bytes 6291488 | tf_op jit(solution)/shard_map/all_to_all | solution.py:82
  821.5 9.7 scatter_custom_fusion.5
  831.2 118.0 %all-to-all-done.7 = f32[8,256,768]{2,1,0:T(8,128)} async-done(((f32[8,256,768]{2,1,0:T(8,128)}), f32[8,256,768]{2,1,0:T(8,128)}, u32[]{:S(2)}, u32[]{:S(2)}) %all-to-all-start.7) | async-done | bytes 6291488 | tf_op jit(solution)/shard_map/all_to_all | solution.py:82
  953.2 9.7 scatter_custom_fusion.7
  962.8 118.3 %all-to-all-done.8 = f32[8,256,768]{2,1,0:T(8,128)} async-done(((f32[8,256,768]{2,1,0:T(8,128)}), f32[8,256,768]{2,1,0:T(8,128)}, u32[]{:S(2)}, u32[]{:S(2)}) %all-to-all-start.8) | async-done | bytes 6291488 | tf_op jit(solution)/shard_map/all_to_all | solution.py:82
  1085.5 9.7 scatter_custom_fusion.9
  1095.1 118.6 %all-to-all-done.9 = f32[8,256,768]{2,1,0:T(8,128)} async-done(((f32[8,256,768]{2,1,0:T(8,128)}), f32[8,256,768]{2,1,0:T(8,128)}, u32[]{:S(2)}, u32[]{:S(2)}) %all-to-all-start.9) | async-done | bytes 6291488 | tf_op jit(solution)/shard_map/all_to_all | solution.py:82
  1217.5 10.0 fusion.241
  1233.6 23.3 scatter_custom_fusion.2
  1256.9 23.2 scatter_custom_fusion.4
  1280.1 22.9 scatter_custom_fusion.6
  1302.9 22.7 scatter_custom_fusion.8
  1325.6 20.7 all-to-all-done.10
  1346.3 23.0 scatter_custom_fusion.10
  1369.3 16.8 bitcast_dynamic-update-slice_fusion.4
  1386.1 16.8 bitcast_dynamic-update-slice_fusion.3
  1403.0 9.7 bitcast_dynamic-update-slice_fusion.2
  1421.0 14.7 bitcast_dynamic-update-slice_fusion
  1435.7 869.8 %all-reduce.3.cloned.1.call-done = (f32[1,768,3072]{2,1,0:T(8,128)}, f32[1,768,3072]{2,1,0:T(8,128)}, f32[1,768,3072]{2,1,0:T(8,128)}, f32[1,768,3072]{2,1,0:T(8...) async-done(((f32[1,768,3072]{2,1,0:T(8,128)}, ...) | async-done | bytes 117964816 | tf_op jit(solution)/shard_map/psum | solution.py:84
  2305.6 8.8 constant_dynamic-update-slice_fusion.4
  2337.2 9.1 constant_dynamic-update-slice_fusion.1
  2356.1 9.1 constant_dynamic-update-slice_fusion.7
  (385 shorter events, 261.3 us)
Async XLA Ops:
  11.4 148.5 %copy-start.83 = (s32[1024]{0:T(1024)}, s32[1024]{0:T(1024)S(1)}, u32[]{:S(2)}) copy-start(s32[1024]{0:T(1024)S(1)} %get-tuple-element.49) | copy-start | bytes 12292
  11.4 492.5 %copy-start.91 = (pred[1024]{0:T(1024)(128)(4,1)}, pred[1024]{0:T(1024)(128)(4,1)S(1)}, u32[]{:S(2)}) copy-start(pred[1024]{0:T(1024)(128)(4,1)S(1)} %get-tuple-element.48) | copy-start | bytes 3076
  16.3 57.7 %all-to-all-start = ((s32[8,256,1]{1,2,0:T(1,128)}), s32[8,256,1]{1,2,0:T(1,128)S(1)}, u32[]{:S(2)}, u32[]{:S(2)}) async-start(s32[8,256,1]{1,2,0:T(1,128)} %bitcast.5), calls=%async_computation | async-start | bytes 16384 | tf_op jit(solution)/shard_map/all_to_all | solution.py:65
  20.6 33.1 %copy-start.56 = (bf16[1024,768]{1,0:T(8,128)(2,1)S(1)}, bf16[1024,768]{1,0:T(8,128)(2,1)}, u32[]{:S(2)}) copy-start(bf16[1024,768]{1,0:T(8,128)(2,1)} %param.13) | copy-start | bytes 4718596
  74.0 13.5 copy-start.77
  157.0 40.8 %all-to-all-start.1 = ((bf16[8,256,768]{2,1,0:T(8,128)(2,1)}), bf16[8,256,768]{2,1,0:T(8,128)(2,1)S(1)}, u32[]{:S(2)}, u32[]{:S(2)}) async-start(bf16[8,256,768]{2,1,0:T(8,128)(2,1)} %bitcast.296), calls=%async_computation.1 | async-start | bytes 6291456 | tf_op jit(solution)/shard_map/all_to_all | solution.py:71
  199.5 40.4 %all-to-all-start.2 = ((bf16[8,256,768]{2,1,0:T(8,128)(2,1)}), bf16[8,256,768]{2,1,0:T(8,128)(2,1)S(1)}, u32[]{:S(2)}, u32[]{:S(2)}) async-start(bf16[8,256,768]{2,1,0:T(8,128)(2,1)} %bitcast.295), calls=%async_computation.2 | async-start | bytes 6291456 | tf_op jit(solution)/shard_map/all_to_all | solution.py:71
  239.8 41.4 %all-to-all-start.3 = ((bf16[8,256,768]{2,1,0:T(8,128)(2,1)}), bf16[8,256,768]{2,1,0:T(8,128)(2,1)}, u32[]{:S(2)}, u32[]{:S(2)}) async-start(bf16[8,256,768]{2,1,0:T(8,128)(2,1)} %bitcast.294), calls=%async_computation.3 | async-start | bytes 6291456 | tf_op jit(solution)/shard_map/all_to_all | solution.py:71
  281.2 40.3 %all-to-all-start.4 = ((bf16[8,256,768]{2,1,0:T(8,128)(2,1)}), bf16[8,256,768]{2,1,0:T(8,128)(2,1)S(1)}, u32[]{:S(2)}, u32[]{:S(2)}) async-start(bf16[8,256,768]{2,1,0:T(8,128)(2,1)} %bitcast.293), calls=%async_computation.4 | async-start | bytes 6291456 | tf_op jit(solution)/shard_map/all_to_all | solution.py:71
  306.4 142.1 %copy-start.87 = (f32[1024]{0:T(1024)}, f32[1024]{0:T(1024)S(1)}, u32[]{:S(2)}) copy-start(f32[1024]{0:T(1024)S(1)} %get-tuple-element.60) | copy-start | bytes 12292
  321.5 40.9 %all-to-all-start.5 = ((bf16[8,256,768]{2,1,0:T(8,128)(2,1)}), bf16[8,256,768]{2,1,0:T(8,128)(2,1)}, u32[]{:S(2)}, u32[]{:S(2)}) async-start(bf16[8,256,768]{2,1,0:T(8,128)(2,1)} %bitcast.292), calls=%async_computation.5 | async-start | bytes 6291456 | tf_op jit(solution)/shard_map/all_to_all | solution.py:71
  324.7 1980.8 %all-reduce.3.cloned.1.call-start = ((), (), s32[]{:S(2)}) async-start(), calls=%async_computation.11 | async-start | bytes 235929600 | tf_op jit(solution)/shard_map/psum | solution.py:84
  344.9 103.6 %copy-start.1 = (bf16[1024,768]{0,1:T(8,128)(2,1)}, bf16[1024,768]{0,1:T(8,128)(2,1)S(1)}, u32[]{:S(2)}) copy-start(bf16[1024,768]{0,1:T(8,128)(2,1)S(1)} %get-tuple-element.78) | copy-start | bytes 4718596
  344.9 103.6 %copy-start.81 = (f32[1024]{0:T(1024)}, f32[1024]{0:T(1024)S(1)}, u32[]{:S(2)}) copy-start(f32[1024]{0:T(1024)S(1)} %get-tuple-element.62) | copy-start | bytes 12292
  370.4 34.9 %slice-start.28 = ((s8[5898240]{0:T(1024)(128)(4,1)}), s8[4194304]{0:T(1024)(128)(4,1)S(1)}, s32[]{:S(2)}) async-start(s8[5898240]{0:T(1024)(128)(4,1)} %bitcast.309), calls=%async_computation.40 | async-start | bytes 8388608
  380.9 24.4 %slice-start.29 = ((s8[5898240]{0:T(1024)(128)(4,1)}), s8[1703936]{0:T(1024)(128)(4,1)S(1)}, s32[]{:S(2)}) async-start(s8[5898240]{0:T(1024)(128)(4,1)} %bitcast.309), calls=%async_computation.41 | async-start | bytes 3407872
  413.0 18.2 copy-start.60
  413.0 18.2 copy-start.46
  413.0 18.2 copy-start.73
  450.1 17.9 copy-start.51
  450.1 17.9 copy-start.42
  450.1 17.9 copy-start.70
  468.0 18.8 slice-start.34
  474.6 12.3 slice-start.35
  486.9 17.0 copy-start.54
  486.9 17.0 copy-start.38
  486.9 17.0 copy-start.67
  547.0 20.7 slice-start.42
  557.4 18.1 slice-start.40
  567.8 15.2 slice-start.30
  575.5 18.6 slice-start.36
  575.5 30.0 %slice-start.38 = ((s8[6291456]{0:T(1024)(128)(4,1)}), s8[4194304]{0:T(1024)(128)(4,1)S(1)}, s32[]{:S(2)}) async-start(s8[6291456]{0:T(1024)(128)(4,1)} %bitcast.327), calls=%async_computation.50 | async-start | bytes 8388608
  583.0 11.1 copy-start.55
  583.0 11.1 slice-start.37
  583.0 22.5 slice-start.39
  594.1 11.4 copy-start.52
  605.5 10.9 copy-start.61
  605.5 24.1 %slice-start.32 = ((s8[6291456]{0:T(1024)(128)(4,1)}), s8[4194304]{0:T(1024)(128)(4,1)S(1)}, s32[]{:S(2)}) async-start(s8[6291456]{0:T(1024)(128)(4,1)} %bitcast.321), calls=%async_computation.44 | async-start | bytes 8388608
  616.4 13.2 copy-start.59
  616.4 13.2 slice-start.33
  686.5 130.8 %all-to-all-start.6 = ((f32[8,256,768]{2,1,0:T(8,128)}), f32[8,256,768]{2,1,0:T(8,128)}, u32[]{:S(2)}, u32[]{:S(2)}) async-start(f32[8,256,768]{2,1,0:T(8,128)} %bitcast.291), calls=%async_computation.6 | async-start | bytes 12582912 | tf_op jit(solution)/shard_map/all_to_all | solution.py:82
  817.3 131.9 %all-to-all-start.7 = ((f32[8,256,768]{2,1,0:T(8,128)}), f32[8,256,768]{2,1,0:T(8,128)}, u32[]{:S(2)}, u32[]{:S(2)}) async-start(f32[8,256,768]{2,1,0:T(8,128)} %bitcast.288), calls=%async_computation.7 | async-start | bytes 12582912 | tf_op jit(solution)/shard_map/all_to_all | solution.py:82
  949.2 132.0 %all-to-all-start.8 = ((f32[8,256,768]{2,1,0:T(8,128)}), f32[8,256,768]{2,1,0:T(8,128)}, u32[]{:S(2)}, u32[]{:S(2)}) async-start(f32[8,256,768]{2,1,0:T(8,128)} %bitcast.289), calls=%async_computation.8 | async-start | bytes 12582912 | tf_op jit(solution)/shard_map/all_to_all | solution.py:82
  1081.2 132.5 %all-to-all-start.9 = ((f32[8,256,768]{2,1,0:T(8,128)}), f32[8,256,768]{2,1,0:T(8,128)}, u32[]{:S(2)}, u32[]{:S(2)}) async-start(f32[8,256,768]{2,1,0:T(8,128)} %bitcast.290), calls=%async_computation.9 | async-start | bytes 12582912 | tf_op jit(solution)/shard_map/all_to_all | solution.py:82
  1213.7 132.6 %all-to-all-start.10 = ((f32[8,256,768]{2,1,0:T(8,128)}), f32[8,256,768]{2,1,0:T(8,128)}, u32[]{:S(2)}, u32[]{:S(2)}) async-start(f32[8,256,768]{2,1,0:T(8,128)} %bitcast.287), calls=%async_computation.10 | async-start | bytes 12582912 | tf_op jit(solution)/shard_map/all_to_all | solution.py:82
  1369.3 33.6 %slice-start.5 = ((s8[19316736]{0:T(1024)(128)(4,1)}), s8[4194304]{0:T(1024)(128)(4,1)S(1)}, s32[]{:S(2)}) async-start(s8[19316736]{0:T(1024)(128)(4,1)} %bitcast.285), calls=%async_computation.17 | async-start | bytes 8388608
  1369.3 33.6 %slice-start.6 = ((s8[19316736]{0:T(1024)(128)(4,1)}), s8[4194304]{0:T(1024)(128)(4,1)S(1)}, s32[]{:S(2)}) async-start(s8[19316736]{0:T(1024)(128)(4,1)} %bitcast.285), calls=%async_computation.18 | async-start | bytes 8388608
  1369.3 33.6 %slice-start.7 = ((s8[19316736]{0:T(1024)(128)(4,1)}), s8[4194304]{0:T(1024)(128)(4,1)S(1)}, s32[]{:S(2)}) async-start(s8[19316736]{0:T(1024)(128)(4,1)} %bitcast.285), calls=%async_computation.19 | async-start | bytes 8388608
  1386.1 16.8 slice-start.8
  1386.1 16.9 slice-start.9
  1386.1 26.6 %slice-start = ((s8[19316736]{0:T(1024)(128)(4,1)}), s8[4194304]{0:T(1024)(128)(4,1)S(1)}, s32[]{:S(2)}) async-start(s8[19316736]{0:T(1024)(128)(4,1)} %bitcast.283), calls=%async_computation.12 | async-start | bytes 8388608
  1386.1 26.6 %slice-start.1 = ((s8[19316736]{0:T(1024)(128)(4,1)}), s8[4194304]{0:T(1024)(128)(4,1)S(1)}, s32[]{:S(2)}) async-start(s8[19316736]{0:T(1024)(128)(4,1)} %bitcast.283), calls=%async_computation.13 | async-start | bytes 8388608
  1386.1 26.6 %slice-start.2 = ((s8[19316736]{0:T(1024)(128)(4,1)}), s8[4194304]{0:T(1024)(128)(4,1)S(1)}, s32[]{:S(2)}) async-start(s8[19316736]{0:T(1024)(128)(4,1)} %bitcast.283), calls=%async_computation.14 | async-start | bytes 8388608
  1402.9 11.0 slice-start.4
  2314.3 11.0 slice-start.25
  2314.3 11.0 slice-start.26
  2331.8 14.5 slice-start.19
  2331.8 14.5 slice-start.20
  2337.2 13.5 slice-start.16
  2337.2 13.5 slice-start.17
  2350.7 14.6 slice-start.13
  2350.7 14.6 slice-start.14
  2356.1 13.5 slice-start.10
  2356.1 13.5 slice-start.11
  (86 other events, 506.7 us)
Sparse Core Ops, SparseCore 0:
  676.8 1628.7 all-reduce.2
where the time goes:
time: 2410 us; the launch traced here: 2400 us
  waiting for transfers between devices  1420 us (59%)
  matrix products  429 us (18%)
  local copies, waits for them, and re-layouts  307 us (13%)
  other arithmetic  183 us (8%)
  starting transfers between devices  39.2 us (2%)
    psum x1, waiting for transfers between devices, device_step(): grads_by_layer[layer_idx] = lax.psum(grads, 'emb')  870 us
    all_to_all x5, waiting for transfers between devices, device_step(): grad_recv = lax.all_to_all(grad_send, 'emb', 0, 0, tiled=True)  493 us
    unnamed x299, local copies, waits for them, and re-layouts  134 us
    scatter-add x5, other arithmetic, device_step(): jax.ops.segment_sum(grad_recv, req_recv, num_segments=rows_dev)  115 us
    gather x5, local copies, waits for them, and re-layouts, device_step(): served = jnp.take(ple_tables[layer_idx], req_recv, axis=0)  73.8 us
    dot_general x4, matrix products, layer_bwd(): jnp.einsum('nd,fd->nf', g_out, down_mat, preferred_element_type=jnp.float32)  68.7 us
    all_to_all x5, waiting for transfers between devices, device_step(): returned = lax.all_to_all(served, 'emb', 0, 0, tiled=True)  60 us
    dot_general x5, matrix products, layer_bwd(): jnp.einsum('nf,nd->fd', act_out, g_out, preferred_element_type=jnp.float32)  56.9 us
  transfers between devices with their start and end apart: 12, of which 11 were waited for; matrix products, arithmetic and copies ran while one was open for 18% of the time, Pallas kernels for 0%

commit v1 on v0

v1 whole, which is shorter than its diff:
```python
import functools

import jax
import jax.numpy as jnp
from jax import lax
from jax.experimental import pallas as pl
from jax.experimental.pallas import tpu as pltpu
from jax.sharding import PartitionSpec as P

EPS = 1e-6
CAP_DIV = 4
CORES = 2
F32 = jnp.float32
BF16 = jnp.bfloat16
GELU_A = 0.7978845608028654
GELU_B = 0.044715 * GELU_A
VMEM_MAX = 67043328
TILE = 512
SPLIT = 3


def nn(a, b):
    return jnp.dot(a, b, preferred_element_type=F32)


def nt(a, b):
    return lax.dot_general(a, b, (((1,), (1,)), ((), ())), preferred_element_type=F32)


def tn(a, b):
    return lax.dot_general(a, b, (((0,), (0,)), ((), ())), preferred_element_type=F32)


def gelu_parts(h):
    sq = h * h
    return 0.5 * jnp.tanh(h * (GELU_B * sq + GELU_A)) + 0.5, sq


def gelu(h):
    return h * gelu_parts(h)[0]


def gelu_slope(h, half, sq):
    return half + (h * (half - half * half)) * ((6 * GELU_B) * sq + 2 * GELU_A)


def norm_rows(x_ref):
    xw = x_ref[...].astype(F32)
    r = lax.rsqrt(jnp.mean(xw * xw, axis=-1, keepdims=True) + EPS)
    return xw, r, (xw * r).astype(BF16)


def token_spec(tile, width):
    return pl.BlockSpec((tile, width), lambda i: (i, 0))


def weight_spec(arr, layer):
    return pl.BlockSpec((None,) + arr.shape[1:], lambda i: (layer, 0, 0), pipeline_mode=pl.Buffered(1))


def fwd_kernel(chunk, x_ref, e_ref, up_ref, down_ref, gate_ref, proj_ref, out_ref):
    xw, _, u = norm_rows(x_ref)
    z = nn(u, gate_ref[...]).astype(BF16).astype(F32)
    s = (gelu(z).astype(BF16).astype(F32) * e_ref[...].astype(F32)).astype(BF16)
    m = None
    for k in range(up_ref.shape[1] // chunk):
        cols = pl.ds(k * chunk, chunk)
        a = gelu(nn(u, up_ref[:, cols]).astype(BF16).astype(F32)).astype(BF16)
        part = nn(a, down_ref[cols, :])
        m = part if m is None else m + part
    q = nn(s, proj_ref[...]).astype(BF16)
    out_ref[...] = (xw + m.astype(BF16).astype(F32) + q.astype(F32)).astype(BF16)


def layer_fwd(layer, x, e, weights, tile=TILE, chunk=1024):
    n, d = x.shape
    f = weights[0].shape[2]
    return pl.pallas_call(
        functools.partial(fwd_kernel, chunk),
        grid=(n // tile,),
        in_specs=[token_spec(tile, d)] * 2 + [weight_spec(w, layer) for w in weights],
        out_specs=token_spec(tile, d),
        out_shape=jax.ShapeDtypeStruct((n, d), BF16),
        compiler_params=pltpu.CompilerParams(vmem_limit_bytes=48 << 20),
        cost_estimate=pl.CostEstimate(flops=4 * n * d * (f + d), bytes_accessed=4 * d * (f + d), transcendentals=n * (f + d)),
        name="layer_fwd",
    )(x, e, *weights)


def gather_kernel(unroll, cnt_ref, idx_ref, table_ref, out_ref, rows, tmp):
    homes, cap = idx_ref.shape
    for h in range(homes):

        def body(t, _, h=h):
            for v in range(unroll):
                j = t * unroll + v
                r = idx_ref[h, j]
                tmp[v] = table_ref[pl.ds(pl.multiple_of(r - (r & 7), 8), 8), :].astype(F32)
                rows[pl.ds(h * cap + j, 1), :] = tmp[v, pl.ds(r & 7, 1), :]
            return 0

        lax.fori_loop(0, (cnt_ref[h] + unroll - 1) // unroll, body, 0)
    out_ref[...] = rows[...].astype(BF16)


def serve_rows(tables, first, count, cnt, idx, unroll=16):
    _, rows, d = tables.shape
    homes, cap = idx.shape
    return pl.pallas_call(
        functools.partial(gather_kernel, unroll),
        grid_spec=pltpu.PrefetchScalarGridSpec(
            num_scalar_prefetch=2,
            grid=(count,),
            in_specs=[pl.BlockSpec((None, rows, d), lambda i, *_: (first + i, 0, 0))],
            out_specs=pl.BlockSpec((None, homes * cap, d), lambda i, *_: (i, 0, 0)),
            scratch_shapes=[pltpu.VMEM((homes * cap, d), F32), pltpu.VMEM((unroll, 8, d), F32)],
        ),
        out_shape=jax.ShapeDtypeStruct((count, homes * cap, d), BF16),
        compiler_params=pltpu.CompilerParams(vmem_limit_bytes=48 << 20),
        cost_estimate=pl.CostEstimate(flops=count * 10**9, bytes_accessed=2 * count * rows * d, transcendentals=0),
        name="serve_rows",
    )(cnt, idx, tables)


def bwd_kernel(chunk, last, seeded, extra, chip_ref, *refs):
    x_ref, e_ref, c_ref, up_ref, down_ref, gate_ref, proj_ref = refs[:7]
    outs = refs[7 + extra:]
    seeds = refs[7:7 + seeded]
    if last:
        gds_ref, gup_ref, gdown_ref, ggate_ref, gproj_ref = outs[:5]
    else:
        cn_ref, gds_ref, gup_ref, gdown_ref, ggate_ref, gproj_ref = outs[:6]
    sem = outs[-1]

    @pl.when(pl.program_id(0) == 0)
    def _():
        accs = (gup_ref, gdown_ref, ggate_ref, gproj_ref)
        if seeded:
            copies = [pltpu.make_async_copy(seeds[k], accs[k], sem.at[k]) for k in range(4)]
            for copy in copies:
                copy.start()
            for copy in copies:
                copy.wait()
        else:
            for ref in accs:
                ref[...] = jnp.zeros_like(ref)

    xw, r, u = norm_rows(x_ref)
    c = c_ref[...].astype(F32)
    o = c.astype(BF16)
    steps = up_ref.shape[1] // chunk

    def first(k):
        cols = pl.ds(k * chunk, chunk)
        return nt(o, down_ref[cols, :]).astype(BF16), nn(u, up_ref[:, cols]).astype(BF16)

    def middle(da, h):
        h = h.astype(F32)
        half, sq = gelu_parts(h)
        return (gelu_slope(h, half, sq) * da.astype(F32)).astype(BF16), (h * half).astype(BF16)

    def final(k, dh, a):
        cols = pl.ds(k * chunk, chunk)
        gup_ref[:, cols] += tn(u, dh)
        gdown_ref[cols, :] += tn(a, o)
        return None if last else nt(dh, up_ref[:, cols])

    pre = first(0)
    z = nn(u, gate_ref[...]).astype(BF16).astype(F32)
    ds = nt(o, proj_ref[...]).astype(BF16).astype(F32)
    e = e_ref[...].astype(F32)
    half, sq = gelu_parts(z)
    g = (z * half).astype(BF16).astype(F32)
    gds_ref[...] = g * ds
    s = (g * e).astype(BF16)
    dz = (gelu_slope(z, half, sq) * (e * ds).astype(BF16).astype(F32)).astype(BF16)
    ggate_ref[...] += tn(u, dz)
    gproj_ref[...] += tn(s, o)
    du = None if last else nt(dz, gate_ref[...])
    mid = None
    for k in range(steps):
        nxt = first(k + 1) if k + 1 < steps else None
        if mid is not None:
            part = final(k - 1, *mid)
            du = None if last else du + part
        mid = middle(*pre)
        pre = nxt
    part = final(steps - 1, *mid)
    if not last:
        du = du + part
        cn_ref[...] = c + r * du - (r * r * r) * xw * jnp.mean(du * xw, axis=-1, keepdims=True)


def layer_bwd(layer, chip, span, total, x, e, c, weights, seed=None, gds=None, c_out=None, c_total=None, tile=TILE, chunk=768):
    d = x[0].shape[1]
    f = weights[0].shape[2]
    last = layer == 0
    struct = jax.ShapeDtypeStruct
    lo, hi = span[0] // tile, span[1] // tile
    block = total // 4 // tile

    def place(kind):
        if kind == "local":
            return pl.BlockSpec((tile, d), lambda i, chip: (i, 0))
        if kind == "ordered":
            return pl.BlockSpec((tile, d), lambda i, chip: (i + lo, 0))

        def index(i, chip):
            t = i + lo
            b = t // block
            b = jnp.where(b == 0, chip[0], jnp.where(b <= chip[0], b - 1, b))
            return (b * block + t % block, 0)

        return pl.BlockSpec((tile, d), index)

    any_spec = pl.BlockSpec(memory_space=pl.ANY)
    wspec = lambda w: pl.BlockSpec((None,) + w.shape[1:], lambda i, chip: (layer, 0, 0), pipeline_mode=pl.Buffered(1))
    whole = lambda shape: pl.BlockSpec(shape, lambda i, chip: (0, 0), pipeline_mode=pl.Buffered(1))
    grads = [(d, f), (f, d), (d, d), (d, d)]
    args = [chip, x[0], e[0], c[0], *weights]
    in_specs = [place(x[1]), place(e[1]), place(c[1])] + [wspec(w) for w in weights]
    aliases = {}
    if seed is not None:
        args += list(seed)
        in_specs += [any_spec] * 4
    n_c = 0 if last else 1
    for buf, pos in ((c_out, 0), (gds, n_c)):
        if buf is not None:
            aliases[len(args)] = pos
            args.append(buf)
            in_specs.append(any_spec)
    rows_out, rows_spec = [], []
    if not last:
        rows_out.append(struct((c_total or (span[1] - span[0]), d), F32))
        rows_spec.append(place("ordered" if c_total else "local"))
    rows_out.append(struct((total, d), F32))
    rows_spec.append(place("ordered"))
    extra = len(args) - 8
    n = span[1] - span[0]
    res = pl.pallas_call(
        functools.partial(bwd_kernel, chunk, last, 0 if seed is None else 4, extra),
        grid_spec=pltpu.PrefetchScalarGridSpec(
            num_scalar_prefetch=1,
            grid=(hi - lo,),
            in_specs=in_specs,
            out_specs=rows_spec + [whole(g) for g in grads],
            scratch_shapes=[pltpu.SemaphoreType.DMA((4,))],
        ),
        out_shape=rows_out + [struct(g, F32) for g in grads],
        input_output_aliases=aliases,
        compiler_params=pltpu.CompilerParams(vmem_limit_bytes=VMEM_MAX),
        cost_estimate=pl.CostEstimate(flops=10 * n * d * (f + d), bytes_accessed=12 * d * (f + d), transcendentals=n * (f + d)),
        name="layer_bwd",
    )(*args)
    return (None if last else res[0]), res[-5], tuple(res[-4:])


def table_kernel(first, layers, seg, unroll, cnt_ref, start_ref, dst_ref, *refs):
    mine, other = refs[:layers], refs[layers:2 * layers]
    out_ref, acc, buf, in_sem, out_sem = refs[-5:]
    homes = dst_ref.shape[0]
    half = homes // 2
    total = mine[0].shape[0]
    toks = total // half

    def base(h):
        return jnp.minimum(start_ref[h] - start_ref[h] % 8, toks - seg)

    def load(l, h):
        ref = mine[l] if h < half else other[l]
        at = pl.multiple_of((h % half) * toks + base(h), 8)
        return pltpu.make_async_copy(ref.at[pl.ds(at, seg), :], buf.at[l % 2, h], in_sem.at[l % 2, h])

    def store(l):
        return pltpu.make_async_copy(acc.at[l % 2], out_ref.at[first - l], out_sem.at[l % 2])

    for h in range(homes):
        load(0, h).start()
    for l in range(layers):
        if l + 1 < layers:
            for h in range(homes):
                load(l + 1, h).start()
        if l >= 2:
            store(l - 2).wait()
        acc[l % 2] = jnp.zeros_like(acc[l % 2])
        for h in range(homes):
            load(l, h).wait()
            off = start_ref[h] - base(h)

            def add(j, h=h, l=l, off=off):
                at = pl.ds(dst_ref[h, j], 1)
                acc[l % 2, at, :] += buf[l % 2, h, pl.ds(off + j, 1), :]

            def many(t, _, add=add):
                for v in range(unroll):
                    add(t * unroll + v)
                return 0

            def one(j, _, add=add):
                add(j)
                return 0

            full = cnt_ref[h] // unroll
            lax.fori_loop(0, full, many, 0)
            lax.fori_loop(full * unroll, cnt_ref[h], one, 0)
        store(l).start()
    for l in range(max(layers - 2, 0), layers):
        store(l).wait()


def table_grad(first, layers_all, rows, cnt, start, dst, mine, other, prev):
    d = mine[0].shape[1]
    homes, cap = dst.shape
    seg = cap + 8
    any_spec = pl.BlockSpec(memory_space=pl.ANY)
    args = [cnt, start, dst, *mine, *other]
    aliases = {}
    if prev is not None:
        aliases = {len(args): 0}
        args.append(prev)
    return pl.pallas_call(
        functools.partial(table_kernel, first, len(mine), seg, 8),
        grid_spec=pltpu.PrefetchScalarGridSpec(
            num_scalar_prefetch=3,
            in_specs=[any_spec] * (len(args) - 3),
            out_specs=any_spec,
            scratch_shapes=[
                pltpu.VMEM((2, rows, d), F32),
                pltpu.VMEM((2, homes, seg, d), F32),
                pltpu.SemaphoreType.DMA((2, homes)),
                pltpu.SemaphoreType.DMA((2,)),
            ],
        ),
        out_shape=jax.ShapeDtypeStruct((layers_all, rows, d), F32),
        input_output_aliases=aliases,
        compiler_params=pltpu.CompilerParams(vmem_limit_bytes=VMEM_MAX),
        cost_estimate=pl.CostEstimate(flops=len(mine) * 10**9, bytes_accessed=8 * len(mine) * rows * d, transcendentals=0),
        name="table_grad",
    )(*args)


def sum_kernel(count, *refs):
    outs = refs[-count:]
    for k in range(count):
        outs[k][...] = refs[k][...] + refs[count + k][...]


def sum_grads(layer, layers, mine, other, prev, steps=8):
    count = len(mine)
    ins, outs = [], []
    for arr in mine:
        block = (arr.shape[0] // steps, arr.shape[1])
        ins.append(pl.BlockSpec(block, lambda i: (i, 0)))
        outs.append(pl.BlockSpec((None,) + block, lambda i: (layer, i, 0)))
    args = list(mine) + list(other)
    aliases = {}
    if prev is not None:
        aliases = {len(args) + k: k for k in range(count)}
        args += list(prev)
    return pl.pallas_call(
        functools.partial(sum_kernel, count),
        grid=(steps,),
        in_specs=ins + ins + [pl.BlockSpec(memory_space=pl.ANY)] * len(aliases),
        out_specs=outs,
        out_shape=[jax.ShapeDtypeStruct((layers,) + arr.shape, F32) for arr in mine],
        input_output_aliases=aliases,
        compiler_params=pltpu.CompilerParams(vmem_limit_bytes=32 << 20),
        cost_estimate=pl.CostEstimate(flops=10**9, bytes_accessed=12 * sum(a.size for a in mine), transcendentals=0),
        name="sum_grads",
    )(*args)


def after(value, *deps):
    return lax.optimization_barrier((value,) + deps)[0]


def solution(mesh):
    shards = mesh.shape["emb"]
    chips = shards // CORES
    same_core = [[chip * CORES + core for chip in range(chips)] for core in range(CORES)]
    swap = [(d, d ^ 1) for d in range(shards)]

    def device_step(tok_ids, x_in, d_out, ple_tables, w_up, w_down, w_gate, w_proj):
        layers, rows_dev, width = ple_tables.shape
        toks = tok_ids.shape[0]
        total = toks * chips
        cap = toks // CAP_DIV
        me = lax.axis_index("emb")
        core, chip = me % CORES, me // CORES
        weights = (w_up, w_down, w_gate, w_proj)
        i32 = jnp.int32

        def gather_core(arr):
            return lax.all_gather(arr, "emb", axis_index_groups=same_core, tiled=True)

        owner = tok_ids // rows_dev
        local_row = tok_ids - owner * rows_dev
        hot = (owner[:, None] == jnp.arange(shards, dtype=i32)[None, :]).astype(i32)
        run = jnp.cumsum(hot, axis=0)
        rank = jnp.sum((run - hot) * hot, axis=1)
        counts = run[-1]
        starts = jnp.cumsum(counts) - counts
        pos = jnp.sum(starts[None, :] * hot, axis=1) + rank
        perm = jnp.zeros((toks,), i32).at[pos].set(jnp.arange(toks, dtype=i32))
        req = jnp.zeros((shards * 2 * cap,), i32).at[owner * (2 * cap) + rank].set(local_row).reshape(shards, 2 * cap)
        req = req.at[:, cap].set(counts).at[:, cap + 1].set(starts)
        req = lax.all_to_all(req, "emb", 0, 0, tiled=True)
        want, cnt, start = req[:, :cap], req[:, cap], req[:, cap + 1]

        x_own = [x_in.at[perm].get(mode="promise_in_bounds")]
        dy_own = d_out.at[perm].get(mode="promise_in_bounds")

        rel = jnp.arange(shards, dtype=i32) ^ me
        cnt_rel, want_rel = cnt[rel], want[rel]
        take = ((owner ^ me) * cap + rank)[perm]

        served = [serve_rows(ple_tables, 0, 1, cnt_rel, want_rel)[0]]
        for l in range(1, layers):
            served.append(serve_rows(ple_tables, l, 1, after(cnt_rel, served[l - 1]), want_rel)[0])
        own_rows = []
        for l in range(layers):
            rows = served[l].reshape(shards, cap, width)
            got = [rows[0]] + [lax.ppermute(rows[s], "emb", [(d, d ^ s) for d in range(shards)]) for s in range(1, shards)]
            if l > 0:
                got[0] = after(got[0], x_own[l])
            own_rows.append(jnp.concatenate(got).at[take].get(mode="promise_in_bounds"))
            x_own.append(layer_fwd(l, x_own[l], own_rows[l], weights))

        chip_arr = chip.astype(i32)[None]
        own, oth, every = (0, toks), (toks, total), (0, total)
        split = layers - SPLIT
        c_own = [None] * (layers + 1)
        c_own[layers] = dy_own
        seeds, gds_buf = {}, {}
        c_rel = None
        for l in reversed(range(split, layers)):
            edge = l == split
            res = layer_bwd(l, chip_arr, own, total, (x_own[l], "local"), (own_rows[l], "local"), (c_own[l + 1], "local"), weights, c_total=total if edge else None)
            c_own[l], gds_buf[l], seeds[l] = res
            if edge:
                c_rel = res[0]
        ready = own_rows[layers - 1]
        dy_all = gather_core(after(dy_own, ready))
        c, kind = after(dy_all, gds_buf[split]), "all"
        gds, part, other = {}, {}, {}
        swapped, sums = {}, None
        for l in reversed(range(layers)):
            e_all = gather_core(after(own_rows[l], ready))
            x_all = gather_core(after(x_own[l], ready))
            xe = ((x_all, "all"), (e_all, "all"))
            if l >= split:
                edge = l == split
                c_new, gds[l], part[l] = layer_bwd(l, chip_arr, oth, total, *xe, (c, kind), weights, seed=seeds[l], gds=gds_buf[l], c_out=c_rel if edge else None, c_total=total if edge else None)
            else:
                c_new, gds[l], part[l] = layer_bwd(l, chip_arr, every, total, *xe, (c, "local"), weights, c_total=total)
            kind = "local"
            swapped[l] = tuple(lax.ppermute(p, "emb", swap) for p in part[l])
            other[l] = lax.ppermute(gds[l], "emb", swap)
            if l + 1 < layers:
                held = lax.optimization_barrier((gds[l], other[l + 1], swapped[l + 1]))
                other[l + 1] = held[1]
                sums = sum_grads(l + 1, layers, part[l + 1], held[2], sums)
                if l > 0:
                    c_new, other[l + 1], sums = lax.optimization_barrier((c_new, other[l + 1], sums))
            c = c_new

        order = jnp.arange(chips, dtype=i32)
        order = jnp.where(order == 0, chip, jnp.where(order <= chip, order - 1, order)) * CORES
        order = jnp.concatenate([order + core, order + 1 - core])
        lists = (cnt[order], start[order], want[order])
        upper = list(range(layers - 1, 0, -1))
        tables = table_grad(layers - 1, layers, rows_dev, *lists, [after(gds[l], gds[0]) for l in upper], [other[l] for l in upper], None)
        sums = sum_grads(0, layers, part[0], after(swapped[0], tables), sums)
        tables = table_grad(0, layers, rows_dev, *lists, [gds[0]], [other[0]], tables)
        x_out = x_own[layers].at[pos].get(mode="promise_in_bounds")
        return (x_out, tables, *sums)

    return jax.shard_map(
        device_step,
        mesh=mesh,
        in_specs=(P("emb"), P("emb", None), P("emb", None), P(None, "emb", None), P(), P(), P(), P()),
        out_specs=(P("emb", None), P(None, "emb", None), P(), P(), P(), P()),
        check_vma=False,
    )
```

time: 2410 us -> 1540 us (0.64)
  waiting for transfers between devices: 1420 us -> 156 us
  Pallas kernels: 0 us -> 1120 us
  matrix products: 429 us -> 0 us
  other arithmetic: 183 us -> 8.13 us
  local copies, waits for them, and re-layouts: 307 us -> 159 us
  starting transfers between devices: 39.2 us -> 66.4 us
    pallas_call x0 -> x25, Pallas kernels: none -> 1120 us  [the longest x8 813 us: layer_bwd(): pl.pallas_call(functools.partial(bwd_kernel, chunk, last, 0 if seed is No...]
    psum x1 -> x0, waiting for transfers between devices: 870 us -> none  [device_step(): grads_by_layer[layer_idx] = lax.psum(grads, 'emb')]
    all_to_all x11 -> x1, waiting for transfers between devices: 553 us -> 0.01 us  [device_step(): req = lax.all_to_all(req, 'emb', 0, 0, tiled=True)]
    dot_general x57 -> x0, matrix products: 429 us -> none  [the longest x4 68.7 us: layer_bwd(): jnp.einsum('nd,fd->nf', g_out, down_mat, preferred_element_type=jnp.float32)]
    scatter-add x5 -> x0, other arithmetic: 115 us -> none  [device_step(): jax.ops.segment_sum(grad_recv, req_recv, num_segments=rows_dev)]
    ppermute x0 -> x60, waiting for transfers between devices: none -> 103 us  [the longest x20 57.4 us: device_step(): swapped[l] = tuple((lax.ppermute(p, 'emb', swap) for p in part[l]))]
    ppermute x0 -> x60, starting transfers between devices: none -> 61.7 us  [the longest x35 55.3 us: device_step(): lax.ppermute(rows[s], 'emb', [(d, d ^ s) for d in range(shards)])]
    unnamed x299 -> x100, local copies, waits for them, and re-layouts: 134 us -> 77.4 us
  transfers between devices with their start and end apart: 12 -> 72, of which waited for: 11 -> 10; matrix products, arithmetic and copies ran while one was open for 18% -> 7% of each run, Pallas kernels for 0% -> 69%
where the time goes in v1:
time: 1540 us; the launch traced here: 1520 us
  Pallas kernels  1120 us (73%)
  local copies, waits for them, and re-layouts  159 us (10%)
  waiting for transfers between devices  156 us (10%)
  starting transfers between devices  66.4 us (4%)
    pallas_call x8, Pallas kernels, layer_bwd(): pl.pallas_call(functools.partial(bwd_kernel, chunk, last, 0 if seed is No...  813 us
    pallas_call x5, Pallas kernels, sum_grads(): pl.pallas_call(functools.partial(sum_kernel, count), grid=(steps,), in_sp...  99.5 us
    pallas_call x5, Pallas kernels, layer_fwd(): pl.pallas_call(functools.partial(fwd_kernel, chunk), grid=(n // tile,), i...  92.9 us
    unnamed x100, local copies, waits for them, and re-layouts  77.4 us
    ppermute x20, waiting for transfers between devices, device_step(): swapped[l] = tuple((lax.ppermute(p, 'emb', swap) for p in part[l]))  57.4 us
    pallas_call x5, Pallas kernels, serve_rows(): pl.pallas_call(functools.partial(gather_kernel, unroll), grid_spec=pltpu....  56.3 us
    ppermute x35, starting transfers between devices, device_step(): lax.ppermute(rows[s], 'emb', [(d, d ^ s) for d in range(shards)])  55.3 us
    pallas_call x2, Pallas kernels, table_grad(): pl.pallas_call(functools.partial(table_kernel, first, len(mine), seg, 8),...  54.9 us
  transfers between devices with their start and end apart: 72, of which 10 were waited for; matrix products, arithmetic and copies ran while one was open for 7% of the time, Pallas kernels for 69%

profile of v1, /device:TPU:0, one launch (start us, length us, event | category | flops | bytes accessed | tf_op | source)
XLA Modules:
  0.0 1520.7 jit_solution(17381979652803131515)
XLA Ops:
  9.3 2.3 reduce-window.10
  13.7 4.3 scatter_custom_fusion.1
  20.3 4.3 all-to-all-start
  24.7 4.3 scatter_custom_fusion
  29.0 4.5 gather_fusion.3
  33.6 4.0 gather_fusion
  37.6 7.7 gather_fusion.13
  47.3 11.1 serve_rows.5
  58.4 11.1 serve_rows.6
  69.6 11.5 serve_rows.7
  81.1 11.1 serve_rows.8
  92.3 11.3 serve_rows.9
  103.8 5.6 collective-permute-start
  111.1 16.7 %collective-permute-start.3 = (bf16[256,768]{1,0:T(8,128)(2,1)S(1)}, bf16[256,768]{1,0:T(8,128)(2,1)S(1)}, u32[]{:S(2)}, u32[]{:S(2)}) collective-permute-start(bf16[256,768]{1,0:T(8,128)(2,1)S(1)} %get-tuple-element.327), channel_id=1, source_target_pairs={{0,4},{1,5},{2,6},{3,7},{4,0},{5,1},{6,2},{7,3}} | collective-permute-start | bytes 1179656 | tf_op jit(solution)/shard_map/ppermute | solution.py:423
  135.2 2.9 collective-permute-start.5
  143.1 20.4 %collective-permute-done.4 = bf16[256,768]{1,0:T(8,128)(2,1)S(1)} collective-permute-done((bf16[256,768]{1,0:T(8,128)(2,1)S(1)}, bf16[256,768]{1,0:T(8,128)(2,1)S(1)}, u32[]{:S(2)}, u32[]{:S(2)}) %collective-permute-start.4) | collective-permute-done | bytes 393248 | tf_op jit(solution)/shard_map/ppermute | solution.py:423
  168.1 6.8 gather_fusion.4
  174.9 18.0 %layer_fwd.5.x_ref = bf16[1024,768]{1,0:T(8,128)(2,1)S(1)} custom-call(bf16[1024,768]{1,0:T(8,128)(2,1)S(1)} %gather_fusion, bf16[1024,768]{1,0:T(8,128)(2,1)S(1)} %gather_fusion.4, bf16[5,768,3072]{2,1,0:T(8,128)(2,1)} %refs_3_.15, bf16[5,3072,768]{2,1,0:T(8,128)(2,1)} %refs_4_.15, bf16[5,768,768]{2,1,0:T(8,128)(2,1)} %refs_5_.15, bf16[5,768,768]{2,1,0:T(8,128)(2,1)} %refs_6_.15), custom_call_target="tpu_custom_call" | custom-call | flops 12079595520 | bytes 11796480 | tf_op jit(solution)/shard_map/layer_fwd/pallas_call | solution.py:78
  197.0 1.8 constant_dynamic-update-slice_fusion.13
  198.7 2.1 collective-permute-start.13
  200.8 1.8 constant_dynamic-update-slice_fusion.12
  202.6 1.8 constant_dynamic-update-slice_fusion.11
  211.7 5.5 collective-permute-done.13
  218.7 6.9 gather_fusion.5
  225.6 18.8 %layer_fwd.6.x_ref.refs_0_ = bf16[1024,768]{1,0:T(8,128)(2,1)} custom-call(bf16[1024,768]{1,0:T(8,128)(2,1)S(1)} %copy-done.7, bf16[1024,768]{1,0:T(8,128)(2,1)S(1)} %gather_fusion.5, bf16[5,768,3072]{2,1,0:T(8,128)(2,1)} %refs_3_.15, bf16[5,3072,768]{2,1,0:T(8,128)(2,1)} %refs_4_.15, bf16[5,768,768]{2,1,0:T(8,128)(2,1)} %refs_5_.15, ...), custom_call_target="tpu_custom_call" | custom-call | flops 12079595520 | bytes 11796480 | tf_op jit(solution)/shard_map/layer_fwd/pallas_call | solution.py:78
  244.5 1.8 constant_dynamic-update-slice_fusion.22
  261.4 4.6 collective-permute-done.20
  266.1 1.8 collective-permute-start.25
  268.7 6.8 gather_fusion.6
  275.5 19.4 %layer_fwd.7.x_ref.refs_0_ = bf16[1024,768]{1,0:T(8,128)(2,1)} custom-call(bf16[1024,768]{1,0:T(8,128)(2,1)} %layer_fwd.6.x_ref.refs_0_, bf16[1024,768]{1,0:T(8,128)(2,1)S(1)} %gather_fusion.6, bf16[5,768,3072]{2,1,0:T(8,128)(2,1)} %refs_3_.15, bf16[5,3072,768]{2,1,0:T(8,128)(2,1)} %refs_4_.15, bf16[5,768,768]{2,1,0:T(8,128)(2,1)} %refs_5_.15, ...), custom_call_target="tpu_custom_call" | custom-call | flops 12079595520 | bytes 11796480 | tf_op jit(solution)/shard_map/layer_fwd/pallas_call | solution.py:78
  310.9 3.9 collective-permute-done.27
  314.7 2.9 collective-permute-start.32
  318.4 6.8 gather_fusion.7
  325.2 19.1 %layer_fwd.8.x_ref.refs_0_ = bf16[1024,768]{1,0:T(8,128)(2,1)} custom-call(bf16[1024,768]{1,0:T(8,128)(2,1)} %layer_fwd.7.x_ref.refs_0_, bf16[1024,768]{1,0:T(8,128)(2,1)S(1)} %gather_fusion.7, bf16[5,768,3072]{2,1,0:T(8,128)(2,1)} %refs_3_.15, bf16[5,3072,768]{2,1,0:T(8,128)(2,1)} %refs_4_.15, bf16[5,768,768]{2,1,0:T(8,128)(2,1)} %refs_5_.15, ...), custom_call_target="tpu_custom_call" | custom-call | flops 12079595520 | bytes 11796480 | tf_op jit(solution)/shard_map/layer_fwd/pallas_call | solution.py:78
  350.9 6.3 collective-permute-done.33
  357.2 4.8 collective-permute-done.34
  362.1 5.3 gather_fusion.8
  371.4 48.6 %layer_bwd.8 = (f32[1024,768]{1,0:T(8,128)}, f32[4096,768]{1,0:T(8,128)}, f32[768,3072]{1,0:T(8,128)}, f32[3072,768]{1,0:T(8,128)}, f32[768,768]{1,0:T(8,128)}, /*index=5*/f32[768,768]{1,0:T(8,128)}) custom-call(s32[1]{0:T(128)} %bitcast.57.chip_ref, bf16[1024,768]{1,0:T(8,128)(2,1)} %layer_fwd.8.x_ref.refs_0_, bf16[1024,768]{1,0:T(8,128)(2,1)} %gather_fusion.8, ...), custom_call_target="tpu_custom_call" | custom-call | flops 30198988800 | bytes 35389440 | tf_op jit(solution)/shard_map/layer_bwd/pallas_call | solution.py:240
  420.0 49.6 %layer_bwd.9 = (f32[1024,768]{1,0:T(8,128)}, f32[4096,768]{1,0:T(8,128)}, f32[768,3072]{1,0:T(8,128)}, f32[3072,768]{1,0:T(8,128)}, f32[768,768]{1,0:T(8,128)}, /*index=5*/f32[768,768]{1,0:T(8,128)}) custom-call(s32[1]{0:T(128)} %bitcast.57.chip_ref, bf16[1024,768]{1,0:T(8,128)(2,1)} %layer_fwd.7.x_ref.refs_0_, bf16[1024,768]{1,0:T(8,128)(2,1)} %copy-done.5, ...), custom_call_target="tpu_custom_call" | custom-call | flops 30198988800 | bytes 35389440 | tf_op jit(solution)/shard_map/layer_bwd/pallas_call | solution.py:240
  469.6 49.7 %layer_bwd.10 = (f32[4096,768]{1,0:T(8,128)}, f32[4096,768]{1,0:T(8,128)}, f32[768,3072]{1,0:T(8,128)}, f32[3072,768]{1,0:T(8,128)}, f32[768,768]{1,0:T(8,128)}, /*index=5*/f32[768,768]{1,0:T(8,128)}) custom-call(s32[1]{0:T(128)} %bitcast.57.chip_ref, bf16[1024,768]{1,0:T(8,128)(2,1)} %layer_fwd.6.x_ref.refs_0_, bf16[1024,768]{1,0:T(8,128)(2,1)} %copy-done.4, ...), custom_call_target="tpu_custom_call" | custom-call | flops 30198988800 | bytes 35389440 | tf_op jit(solution)/shard_map/layer_bwd/pallas_call | solution.py:240
  519.5 45.8 %all-gather.30.cloned.1.call-done.refs_1_ = bf16[4096,768]{1,0:T(8,128)(2,1)} async-done(((bf16[1024,768]{1,0:T(8,128)(2,1)}), bf16[4096,768]{1,0:T(8,128)(2,1)}) %all-gather.30.cloned.1.call-update) | async-done | bytes 6291472 | tf_op jit(solution)/shard_map/all_gather | solution.py:394
  565.3 127.4 %layer_bwd.11 = (f32[3072,768]{1,0:T(8,128)}, f32[4096,768]{1,0:T(8,128)}, f32[768,3072]{1,0:T(8,128)}, f32[3072,768]{1,0:T(8,128)}, f32[768,768]{1,0:T(8,128)}, /*index=5*/f32[768,768]{1,0:T(8,128)}) custom-call(s32[1]{0:T(128)} %bitcast.57.chip_ref, bf16[4096,768]{1,0:T(8,128)(2,1)} %all-gather.28.cloned.1.call-done.refs_0_, ...), custom_call_target="tpu_custom_call", output_to_operand_aliasing={{1}: (12, {})} | custom-call | flops 90596966400 | bytes 35389440 | tf_op jit(solution)/shard_map/layer_bwd/pallas_call | solution.py:240
  693.9 3.4 all-gather.24.cloned.1.call-done.refs_0_
  697.3 127.6 %layer_bwd.12 = (f32[3072,768]{1,0:T(8,128)}, f32[4096,768]{1,0:T(8,128)}, f32[768,3072]{1,0:T(8,128)}, f32[3072,768]{1,0:T(8,128)}, f32[768,768]{1,0:T(8,128)}, /*index=5*/f32[768,768]{1,0:T(8,128)}) custom-call(s32[1]{0:T(128)} %bitcast.57.chip_ref, bf16[4096,768]{1,0:T(8,128)(2,1)} %all-gather.24.cloned.1.call-done.refs_0_, ...), custom_call_target="tpu_custom_call", output_to_operand_aliasing={{1}: (12, {})} | custom-call | flops 90596966400 | bytes 35389440 | tf_op jit(solution)/shard_map/layer_bwd/pallas_call | solution.py:240
  825.5 21.9 %collective-permute-done.39.refs_7_ = f32[768,768]{1,0:T(8,128)S(1)} collective-permute-done((f32[768,768]{1,0:T(8,128)}, f32[768,768]{1,0:T(8,128)S(1)}, u32[]{:S(2)}, u32[]{:S(2)}) %collective-permute-start.39) | collective-permute-done | bytes 2359328 | tf_op jit(solution)/shard_map/ppermute | solution.py:457
  848.5 3.7 copy-done.13
  855.5 18.8 %sum_grads.5 = (f32[5,768,3072]{2,1,0:T(8,128)}, f32[5,3072,768]{2,1,0:T(8,128)}, f32[5,768,768]{2,1,0:T(8,128)}, f32[5,768,768]{2,1,0:T(8,128)}) custom-call(f32[768,3072]{1,0:T(8,128)S(1)} %copy-done.13, f32[3072,768]{1,0:T(8,128)} %get-tuple-element.193.refs_1_, f32[768,768]{1,0:T(8,128)S(1)} %copy-done.14, f32[768,768]{1,0:T(8,128)S(1)} %copy-done.15, ...), custom_call_target="tpu_custom_call" | custom-call | flops 1000000000 | bytes 70778880 | tf_op jit(solution)/shard_map/sum_grads/pallas_call | solution.py:360
  874.3 127.2 %layer_bwd.13 = (f32[4096,768]{1,0:T(8,128)}, f32[4096,768]{1,0:T(8,128)}, f32[768,3072]{1,0:T(8,128)}, f32[3072,768]{1,0:T(8,128)}, f32[768,768]{1,0:T(8,128)}, /*index=5*/f32[768,768]{1,0:T(8,128)}) custom-call(s32[1]{0:T(128)} %bitcast.57.chip_ref, ...), custom_call_target="tpu_custom_call", output_to_operand_aliasing={{0}: (12, {}), {1}: (13, {})} | custom-call | flops 90596966400 | bytes 35389440 | tf_op jit(solution)/shard_map/layer_bwd/pallas_call | solution.py:240
  1001.8 3.7 copy-done.12
  1008.8 19.2 %sum_grads.6 = (f32[5,768,3072]{2,1,0:T(8,128)}, f32[5,3072,768]{2,1,0:T(8,128)}, f32[5,768,768]{2,1,0:T(8,128)}, f32[5,768,768]{2,1,0:T(8,128)}) custom-call(f32[768,3072]{1,0:T(8,128)S(1)} %copy-done.12, f32[3072,768]{1,0:T(8,128)} %get-tuple-element.214.refs_1_, ...), custom_call_target="tpu_custom_call", output_to_operand_aliasing={{0}: (8, {}), {1}: (9, {}), {2}: (10, {}), {3}: (11, {})} | custom-call | flops 1000000000 | bytes 70778880 | tf_op jit(solution)/shard_map/sum_grads/pallas_call | solution.py:360
  1029.0 155.5 %layer_bwd.14 = (f32[4096,768]{1,0:T(8,128)}, f32[4096,768]{1,0:T(8,128)}, f32[768,3072]{1,0:T(8,128)}, f32[3072,768]{1,0:T(8,128)}, f32[768,768]{1,0:T(8,128)}, /*index=5*/f32[768,768]{1,0:T(8,128)}) custom-call(s32[1]{0:T(128)} %bitcast.57.chip_ref, bf16[4096,768]{1,0:T(8,128)(2,1)} %all-gather.16.cloned.1.call-done.refs_0_, ...), custom_call_target="tpu_custom_call" | custom-call | flops 120795955200 | bytes 35389440 | tf_op jit(solution)/shard_map/layer_bwd/pallas_call | solution.py:240
  1185.5 23.6 %sum_grads.7 = (f32[5,768,3072]{2,1,0:T(8,128)}, f32[5,3072,768]{2,1,0:T(8,128)}, f32[5,768,768]{2,1,0:T(8,128)}, f32[5,768,768]{2,1,0:T(8,128)}) custom-call(f32[768,3072]{1,0:T(8,128)} %get-tuple-element.233.refs_0_, f32[3072,768]{1,0:T(8,128)} %get-tuple-element.234.refs_1_, ...), custom_call_target="tpu_custom_call", output_to_operand_aliasing={{0}: (8, {}), {1}: (9, {}), {2}: (10, {}), {3}: (11, {})} | custom-call | flops 1000000000 | bytes 70778880 | tf_op jit(solution)/shard_map/sum_grads/pallas_call | solution.py:360
  1209.1 127.0 %layer_bwd.15 = (f32[4096,768]{1,0:T(8,128)}, f32[768,3072]{1,0:T(8,128)}, f32[3072,768]{1,0:T(8,128)}, f32[768,768]{1,0:T(8,128)}, f32[768,768]{1,0:T(8,128)}) custom-call(s32[1]{0:T(128)} %bitcast.57.chip_ref, bf16[4096,768]{1,0:T(8,128)(2,1)} %all-gather.12.cloned.1.call-done.refs_0_, bf16[4096,768]{1,0:T(8,128)(2,1)} %all-gather.14.cloned.1.call-done.refs_1_, ...), custom_call_target="tpu_custom_call" | custom-call | flops 120795955200 | bytes 35389440 | tf_op jit(solution)/shard_map/layer_bwd/pallas_call | solution.py:240
  1336.7 35.4 %collective-permute-done.55.refs_7_ = f32[768,768]{1,0:T(8,128)S(1)} collective-permute-done((f32[768,768]{1,0:T(8,128)}, f32[768,768]{1,0:T(8,128)S(1)}, u32[]{:S(2)}, u32[]{:S(2)}) %collective-permute-start.55) | collective-permute-done | bytes 2359328 | tf_op jit(solution)/shard_map/ppermute | solution.py:457
  1375.3 1.8 gather_fusion.12
  1377.2 1.9 gather_fusion.10
  1382.2 17.6 %layer_fwd.9 = bf16[1024,768]{1,0:T(8,128)(2,1)S(1)} custom-call(bf16[1024,768]{1,0:T(8,128)(2,1)} %layer_fwd.8.x_ref.refs_0_, bf16[1024,768]{1,0:T(8,128)(2,1)S(1)} %copy-done.3, bf16[5,768,3072]{2,1,0:T(8,128)(2,1)} %refs_3_.15, bf16[5,3072,768]{2,1,0:T(8,128)(2,1)} %refs_4_.15, bf16[5,768,768]{2,1,0:T(8,128)(2,1)} %refs_5_.15, bf16[5,768,768]{2,1,0:T(8,128)(2,1)} %refs_6_.15), custom_call_target="tpu_custom_call" | custom-call | flops 12079595520 | bytes 11796480 | tf_op jit(solution)/shard_map/layer_fwd/pallas_call | solution.py:78
  1399.9 5.2 gather_fusion.9
  1405.1 3.7 copy-done.10
  1413.7 18.8 %sum_grads.8 = (f32[5,768,3072]{2,1,0:T(8,128)}, f32[5,3072,768]{2,1,0:T(8,128)}, f32[5,768,768]{2,1,0:T(8,128)}, f32[5,768,768]{2,1,0:T(8,128)}) custom-call(f32[768,3072]{1,0:T(8,128)S(1)} %copy-done.10, f32[3072,768]{1,0:T(8,128)} %get-tuple-element.260.refs_1_, ...), custom_call_target="tpu_custom_call", output_to_operand_aliasing={{0}: (8, {}), {1}: (9, {}), {2}: (10, {}), {3}: (11, {})} | custom-call | flops 1000000000 | bytes 70778880 | tf_op jit(solution)/shard_map/sum_grads/pallas_call | solution.py:360
  1432.5 39.8 %table_grad.2.refs_2_ = f32[5,6288,768]{2,1,0:T(8,128)} custom-call(s32[8]{0:T(128)} %gather_fusion.10, s32[8]{0:T(128)} %gather_fusion.11, s32[8,256]{1,0:T(8,128)} %gather_fusion.12, f32[4096,768]{1,0:T(8,128)} %get-tuple-element.252.refs_0_, f32[4096,768]{1,0:T(8,128)} %get-tuple-element.253.refs_1_, f32[4096,768]{1,0:T(8,128)} %get-tuple-element.254.refs_2_, ...), custom_call_target="tpu_custom_call" | custom-call | flops 4000000000 | bytes 154533888 | tf_op jit(solution)/shard_map/table_grad/pallas_call | solution.py:321
  1472.3 3.7 copy-done.11
  1479.3 19.2 %sum_grads.9 = (f32[5,768,3072]{2,1,0:T(8,128)}, f32[5,3072,768]{2,1,0:T(8,128)}, f32[5,768,768]{2,1,0:T(8,128)}, f32[5,768,768]{2,1,0:T(8,128)}) custom-call(f32[768,3072]{1,0:T(8,128)S(1)} %copy-done.11, f32[3072,768]{1,0:T(8,128)} %get-tuple-element.265.refs_1_, ...), custom_call_target="tpu_custom_call", output_to_operand_aliasing={{0}: (8, {}), {1}: (9, {}), {2}: (10, {}), {3}: (11, {})} | custom-call | flops 1000000000 | bytes 70778880 | tf_op jit(solution)/shard_map/sum_grads/pallas_call | solution.py:360
  1498.6 15.1 table_grad.3
  (276 shorter events, 110.5 us)
Async XLA Ops:
  20.3 25.1 %all-to-all-start = ((s32[8,1,512]{2,1,0:T(1,128)}), s32[8,1,512]{2,1,0:T(1,128)S(1)}, u32[]{:S(2)}, u32[]{:S(2)}) async-start(s32[8,1,512]{2,1,0:T(1,128)} %copy.50), calls=%async_computation | async-start | bytes 32768 | tf_op jit(solution)/shard_map/all_to_all | solution.py:407
  24.6 494.9 %all-gather.32.cloned.1.call-start = ((), (), s32[]{:S(2)}) async-start(), calls=%async_computation.11 | async-start | bytes 7864320 | tf_op jit(solution)/shard_map/all_gather | solution.py:394
  103.8 31.4 %collective-permute-start = (bf16[256,768]{1,0:T(8,128)(2,1)S(1)}, bf16[256,768]{1,0:T(8,128)(2,1)S(1)}, u32[]{:S(2)}, u32[]{:S(2)}) collective-permute-start(bf16[256,768]{1,0:T(8,128)(2,1)S(1)} %get-tuple-element.330), channel_id=1, source_target_pairs={{0,1},{1,0},{2,3},{3,2},{4,5},{5,4},{6,7},{7,6}} | collective-permute-start | bytes 1179656 | tf_op jit(solution)/shard_map/ppermute | solution.py:423
  109.4 29.5 %collective-permute-start.1 = (bf16[256,768]{1,0:T(8,128)(2,1)S(1)}, bf16[256,768]{1,0:T(8,128)(2,1)S(1)}, u32[]{:S(2)}, u32[]{:S(2)}) collective-permute-start(bf16[256,768]{1,0:T(8,128)(2,1)S(1)} %get-tuple-element.329), channel_id=1, source_target_pairs={{0,2},{1,3},{2,0},{3,1},{4,6},{5,7},{6,4},{7,5}} | collective-permute-start | bytes 1179656 | tf_op jit(solution)/shard_map/ppermute | solution.py:423
  111.1 28.6 %collective-permute-start.2 = (bf16[256,768]{1,0:T(8,128)(2,1)S(1)}, bf16[256,768]{1,0:T(8,128)(2,1)S(1)}, u32[]{:S(2)}, u32[]{:S(2)}) collective-permute-start(bf16[256,768]{1,0:T(8,128)(2,1)S(1)} %get-tuple-element.328), channel_id=1, source_target_pairs={{0,3},{1,2},{2,1},{3,0},{4,7},{5,6},{6,5},{7,4}} | collective-permute-start | bytes 1179656 | tf_op jit(solution)/shard_map/ppermute | solution.py:423
  111.1 29.7 %collective-permute-start.3 = (bf16[256,768]{1,0:T(8,128)(2,1)S(1)}, bf16[256,768]{1,0:T(8,128)(2,1)S(1)}, u32[]{:S(2)}, u32[]{:S(2)}) collective-permute-start(bf16[256,768]{1,0:T(8,128)(2,1)S(1)} %get-tuple-element.327), channel_id=1, source_target_pairs={{0,4},{1,5},{2,6},{3,7},{4,0},{5,1},{6,2},{7,3}} | collective-permute-start | bytes 1179656 | tf_op jit(solution)/shard_map/ppermute | solution.py:423
  135.2 28.3 %collective-permute-start.4 = (bf16[256,768]{1,0:T(8,128)(2,1)S(1)}, bf16[256,768]{1,0:T(8,128)(2,1)S(1)}, u32[]{:S(2)}, u32[]{:S(2)}) collective-permute-start(bf16[256,768]{1,0:T(8,128)(2,1)S(1)} %get-tuple-element.326), channel_id=1, source_target_pairs={{0,5},{1,4},{2,7},{3,6},{4,1},{5,0},{6,3},{7,2}} | collective-permute-start | bytes 1179656 | tf_op jit(solution)/shard_map/ppermute | solution.py:423
  135.2 30.2 %collective-permute-start.5 = (bf16[256,768]{1,0:T(8,128)(2,1)S(1)}, bf16[256,768]{1,0:T(8,128)(2,1)S(1)}, u32[]{:S(2)}, u32[]{:S(2)}) collective-permute-start(bf16[256,768]{1,0:T(8,128)(2,1)S(1)} %get-tuple-element.325), channel_id=1, source_target_pairs={{0,6},{1,7},{2,4},{3,5},{4,2},{5,3},{6,0},{7,1}} | collective-permute-start | bytes 1179656 | tf_op jit(solution)/shard_map/ppermute | solution.py:423
  138.9 28.4 %collective-permute-start.6 = (bf16[256,768]{1,0:T(8,128)(2,1)S(1)}, bf16[256,768]{1,0:T(8,128)(2,1)S(1)}, u32[]{:S(2)}, u32[]{:S(2)}) collective-permute-start(bf16[256,768]{1,0:T(8,128)(2,1)S(1)} %get-tuple-element.324), channel_id=1, source_target_pairs={{0,7},{1,6},{2,5},{3,4},{4,3},{5,2},{6,1},{7,0}} | collective-permute-start | bytes 1179656 | tf_op jit(solution)/shard_map/ppermute | solution.py:423
  139.7 56.1 %collective-permute-start.7 = (bf16[256,768]{1,0:T(8,128)(2,1)}, bf16[256,768]{1,0:T(8,128)(2,1)}, u32[]{:S(2)}, u32[]{:S(2)}) collective-permute-start(bf16[256,768]{1,0:T(8,128)(2,1)} %get-tuple-element.322), channel_id=1, source_target_pairs={{0,1},{1,0},{2,3},{3,2},{4,5},{5,4},{6,7},{7,6}} | collective-permute-start | bytes 1179656 | tf_op jit(solution)/shard_map/ppermute | solution.py:423
  140.8 57.9 %collective-permute-start.8 = (bf16[256,768]{1,0:T(8,128)(2,1)}, bf16[256,768]{1,0:T(8,128)(2,1)}, u32[]{:S(2)}, u32[]{:S(2)}) collective-permute-start(bf16[256,768]{1,0:T(8,128)(2,1)} %get-tuple-element.321), channel_id=1, source_target_pairs={{0,2},{1,3},{2,0},{3,1},{4,6},{5,7},{6,4},{7,5}} | collective-permute-start | bytes 1179656 | tf_op jit(solution)/shard_map/ppermute | solution.py:423
  163.5 39.2 %collective-permute-start.9 = (bf16[256,768]{1,0:T(8,128)(2,1)}, bf16[256,768]{1,0:T(8,128)(2,1)}, u32[]{:S(2)}, u32[]{:S(2)}) collective-permute-start(bf16[256,768]{1,0:T(8,128)(2,1)} %get-tuple-element.320), channel_id=1, source_target_pairs={{0,3},{1,2},{2,1},{3,0},{4,7},{5,6},{6,5},{7,4}} | collective-permute-start | bytes 1179656 | tf_op jit(solution)/shard_map/ppermute | solution.py:423
  165.5 38.9 %collective-permute-start.10 = (bf16[256,768]{1,0:T(8,128)(2,1)}, bf16[256,768]{1,0:T(8,128)(2,1)}, u32[]{:S(2)}, u32[]{:S(2)}) collective-permute-start(bf16[256,768]{1,0:T(8,128)(2,1)} %get-tuple-element.319), channel_id=1, source_target_pairs={{0,4},{1,5},{2,6},{3,7},{4,0},{5,1},{6,2},{7,3}} | collective-permute-start | bytes 1179656 | tf_op jit(solution)/shard_map/ppermute | solution.py:423
  167.3 39.8 %collective-permute-start.11 = (bf16[256,768]{1,0:T(8,128)(2,1)}, bf16[256,768]{1,0:T(8,128)(2,1)}, u32[]{:S(2)}, u32[]{:S(2)}) collective-permute-start(bf16[256,768]{1,0:T(8,128)(2,1)} %get-tuple-element.318), channel_id=1, source_target_pairs={{0,5},{1,4},{2,7},{3,6},{4,1},{5,0},{6,3},{7,2}} | collective-permute-start | bytes 1179656 | tf_op jit(solution)/shard_map/ppermute | solution.py:423
  202.6 43.7 %collective-permute-start.14 = (bf16[256,768]{1,0:T(8,128)(2,1)}, bf16[256,768]{1,0:T(8,128)(2,1)}, u32[]{:S(2)}, u32[]{:S(2)}) collective-permute-start(bf16[256,768]{1,0:T(8,128)(2,1)} %get-tuple-element.314), channel_id=1, source_target_pairs={{0,1},{1,0},{2,3},{3,2},{4,5},{5,4},{6,7},{7,6}} | collective-permute-start | bytes 1179656 | tf_op jit(solution)/shard_map/ppermute | solution.py:423
  204.4 44.9 %collective-permute-start.15 = (bf16[256,768]{1,0:T(8,128)(2,1)}, bf16[256,768]{1,0:T(8,128)(2,1)}, u32[]{:S(2)}, u32[]{:S(2)}) collective-permute-start(bf16[256,768]{1,0:T(8,128)(2,1)} %get-tuple-element.313), channel_id=1, source_target_pairs={{0,2},{1,3},{2,0},{3,1},{4,6},{5,7},{6,4},{7,5}} | collective-permute-start | bytes 1179656 | tf_op jit(solution)/shard_map/ppermute | solution.py:423
  207.1 45.2 %collective-permute-start.16 = (bf16[256,768]{1,0:T(8,128)(2,1)}, bf16[256,768]{1,0:T(8,128)(2,1)}, u32[]{:S(2)}, u32[]{:S(2)}) collective-permute-start(bf16[256,768]{1,0:T(8,128)(2,1)} %get-tuple-element.312), channel_id=1, source_target_pairs={{0,3},{1,2},{2,1},{3,0},{4,7},{5,6},{6,5},{7,4}} | collective-permute-start | bytes 1179656 | tf_op jit(solution)/shard_map/ppermute | solution.py:423
  209.8 44.9 %collective-permute-start.17 = (bf16[256,768]{1,0:T(8,128)(2,1)}, bf16[256,768]{1,0:T(8,128)(2,1)}, u32[]{:S(2)}, u32[]{:S(2)}) collective-permute-start(bf16[256,768]{1,0:T(8,128)(2,1)} %get-tuple-element.311), channel_id=1, source_target_pairs={{0,4},{1,5},{2,6},{3,7},{4,0},{5,1},{6,2},{7,3}} | collective-permute-start | bytes 1179656 | tf_op jit(solution)/shard_map/ppermute | solution.py:423
  217.2 39.6 %collective-permute-start.18 = (bf16[256,768]{1,0:T(8,128)(2,1)}, bf16[256,768]{1,0:T(8,128)(2,1)}, u32[]{:S(2)}, u32[]{:S(2)}) collective-permute-start(bf16[256,768]{1,0:T(8,128)(2,1)} %get-tuple-element.310), channel_id=1, source_target_pairs={{0,5},{1,4},{2,7},{3,6},{4,1},{5,0},{6,3},{7,2}} | collective-permute-start | bytes 1179656 | tf_op jit(solution)/shard_map/ppermute | solution.py:423
  252.3 43.4 %collective-permute-start.21 = (bf16[256,768]{1,0:T(8,128)(2,1)}, bf16[256,768]{1,0:T(8,128)(2,1)}, u32[]{:S(2)}, u32[]{:S(2)}) collective-permute-start(bf16[256,768]{1,0:T(8,128)(2,1)} %get-tuple-element.306), channel_id=1, source_target_pairs={{0,1},{1,0},{2,3},{3,2},{4,5},{5,4},{6,7},{7,6}} | collective-permute-start | bytes 1179656 | tf_op jit(solution)/shard_map/ppermute | solution.py:423
  254.7 43.7 %collective-permute-start.22 = (bf16[256,768]{1,0:T(8,128)(2,1)}, bf16[256,768]{1,0:T(8,128)(2,1)}, u32[]{:S(2)}, u32[]{:S(2)}) collective-permute-start(bf16[256,768]{1,0:T(8,128)(2,1)} %get-tuple-element.305), channel_id=1, source_target_pairs={{0,2},{1,3},{2,0},{3,1},{4,6},{5,7},{6,4},{7,5}} | collective-permute-start | bytes 1179656 | tf_op jit(solution)/shard_map/ppermute | solution.py:423
  256.7 44.6 %collective-permute-start.23 = (bf16[256,768]{1,0:T(8,128)(2,1)}, bf16[256,768]{1,0:T(8,128)(2,1)}, u32[]{:S(2)}, u32[]{:S(2)}) collective-permute-start(bf16[256,768]{1,0:T(8,128)(2,1)} %get-tuple-element.304), channel_id=1, source_target_pairs={{0,3},{1,2},{2,1},{3,0},{4,7},{5,6},{6,5},{7,4}} | collective-permute-start | bytes 1179656 | tf_op jit(solution)/shard_map/ppermute | solution.py:423
  259.6 44.5 %collective-permute-start.24 = (bf16[256,768]{1,0:T(8,128)(2,1)}, bf16[256,768]{1,0:T(8,128)(2,1)}, u32[]{:S(2)}, u32[]{:S(2)}) collective-permute-start(bf16[256,768]{1,0:T(8,128)(2,1)} %get-tuple-element.303), channel_id=1, source_target_pairs={{0,4},{1,5},{2,6},{3,7},{4,0},{5,1},{6,2},{7,3}} | collective-permute-start | bytes 1179656 | tf_op jit(solution)/shard_map/ppermute | solution.py:423
  266.1 40.7 %collective-permute-start.25 = (bf16[256,768]{1,0:T(8,128)(2,1)S(1)}, bf16[256,768]{1,0:T(8,128)(2,1)}, u32[]{:S(2)}, u32[]{:S(2)}) collective-permute-start(bf16[256,768]{1,0:T(8,128)(2,1)S(1)} %copy-done.30), channel_id=1, source_target_pairs={{0,5},{1,4},{2,7},{3,6},{4,1},{5,0},{6,3},{7,2}} | collective-permute-start | bytes 1179656 | tf_op jit(solution)/shard_map/ppermute | solution.py:423
  301.3 43.0 %collective-permute-start.28 = (bf16[256,768]{1,0:T(8,128)(2,1)}, bf16[256,768]{1,0:T(8,128)(2,1)}, u32[]{:S(2)}, u32[]{:S(2)}) collective-permute-start(bf16[256,768]{1,0:T(8,128)(2,1)} %get-tuple-element.298), channel_id=1, source_target_pairs={{0,1},{1,0},{2,3},{3,2},{4,5},{5,4},{6,7},{7,6}} | collective-permute-start | bytes 1179656 | tf_op jit(solution)/shard_map/ppermute | solution.py:423
  304.0 42.5 %collective-permute-start.29 = (bf16[256,768]{1,0:T(8,128)(2,1)}, bf16[256,768]{1,0:T(8,128)(2,1)}, u32[]{:S(2)}, u32[]{:S(2)}) collective-permute-start(bf16[256,768]{1,0:T(8,128)(2,1)} %get-tuple-element.297), channel_id=1, source_target_pairs={{0,2},{1,3},{2,0},{3,1},{4,6},{5,7},{6,4},{7,5}} | collective-permute-start | bytes 1179656 | tf_op jit(solution)/shard_map/ppermute | solution.py:423
  306.7 41.1 %collective-permute-start.30 = (bf16[256,768]{1,0:T(8,128)(2,1)}, bf16[256,768]{1,0:T(8,128)(2,1)}, u32[]{:S(2)}, u32[]{:S(2)}) collective-permute-start(bf16[256,768]{1,0:T(8,128)(2,1)} %get-tuple-element.296), channel_id=1, source_target_pairs={{0,3},{1,2},{2,1},{3,0},{4,7},{5,6},{6,5},{7,4}} | collective-permute-start | bytes 1179656 | tf_op jit(solution)/shard_map/ppermute | solution.py:423
  308.9 40.0 %collective-permute-start.31 = (bf16[256,768]{1,0:T(8,128)(2,1)}, bf16[256,768]{1,0:T(8,128)(2,1)}, u32[]{:S(2)}, u32[]{:S(2)}) collective-permute-start(bf16[256,768]{1,0:T(8,128)(2,1)} %get-tuple-element.295), channel_id=1, source_target_pairs={{0,4},{1,5},{2,6},{3,7},{4,0},{5,1},{6,2},{7,3}} | collective-permute-start | bytes 1179656 | tf_op jit(solution)/shard_map/ppermute | solution.py:423
  314.7 35.2 %collective-permute-start.32 = (bf16[256,768]{1,0:T(8,128)(2,1)}, bf16[256,768]{1,0:T(8,128)(2,1)}, u32[]{:S(2)}, u32[]{:S(2)}) collective-permute-start(bf16[256,768]{1,0:T(8,128)(2,1)} %get-tuple-element.294), channel_id=1, source_target_pairs={{0,5},{1,4},{2,7},{3,6},{4,1},{5,0},{6,3},{7,2}} | collective-permute-start | bytes 1179656 | tf_op jit(solution)/shard_map/ppermute | solution.py:423
  367.4 152.1 %all-gather.28.cloned.1.call-start = ((), (), s32[]{:S(2)}) async-start(), calls=%async_computation.9 | async-start | bytes 7864320 | tf_op jit(solution)/shard_map/all_gather | solution.py:394
  368.1 197.2 %all-gather.30.cloned.1.call-start = ((), (), s32[]{:S(2)}) async-start(), calls=%async_computation.10 | async-start | bytes 7864320 | tf_op jit(solution)/shard_map/all_gather | solution.py:394
  368.9 325.0 %all-gather.26.cloned.1.call-start = ((), (), s32[]{:S(2)}) async-start(), calls=%async_computation.8 | async-start | bytes 7864320 | tf_op jit(solution)/shard_map/all_gather | solution.py:394
  369.4 327.8 %all-gather.24.cloned.1.call-start = ((), (), s32[]{:S(2)}) async-start(), calls=%async_computation.7 | async-start | bytes 7864320 | tf_op jit(solution)/shard_map/all_gather | solution.py:394
  370.0 504.3 %all-gather.22.cloned.1.call-start = ((), (), s32[]{:S(2)}) async-start(), calls=%async_computation.6 | async-start | bytes 7864320 | tf_op jit(solution)/shard_map/all_gather | solution.py:394
  370.6 503.7 %all-gather.20.cloned.1.call-start = ((), (), s32[]{:S(2)}) async-start(), calls=%async_computation.5 | async-start | bytes 7864320 | tf_op jit(solution)/shard_map/all_gather | solution.py:394
  371.4 657.7 %all-gather.18.cloned.1.call-start = ((), (), s32[]{:S(2)}) async-start(), calls=%async_computation.4 | async-start | bytes 7864320 | tf_op jit(solution)/shard_map/all_gather | solution.py:394
  519.4 509.6 %all-gather.16.cloned.1.call-start = ((), (), s32[]{:S(2)}) async-start(), calls=%async_computation.3 | async-start | bytes 7864320 | tf_op jit(solution)/shard_map/all_gather | solution.py:394
  692.7 155.4 %collective-permute-start.35 = (f32[4096,768]{1,0:T(8,128)}, f32[4096,768]{1,0:T(8,128)}, u32[]{:S(2)}, u32[]{:S(2)}) collective-permute-start(f32[4096,768]{1,0:T(8,128)} %get-tuple-element.252.refs_0_), channel_id=1, source_target_pairs={{0,1},{1,0},{2,3},{3,2},{4,5},{5,4},{6,7},{7,6}} | collective-permute-start | bytes 37748744 | tf_op jit(solution)/shard_map/ppermute | solution.py:458
  692.8 516.3 %all-gather.14.cloned.1.call-start = ((), (), s32[]{:S(2)}) async-start(), calls=%async_computation.2 | async-start | bytes 7864320 | tf_op jit(solution)/shard_map/all_gather | solution.py:394
  692.8 154.8 %collective-permute-start.36 = (f32[768,3072]{1,0:T(8,128)}, f32[768,3072]{1,0:T(8,128)}, u32[]{:S(2)}, u32[]{:S(2)}) collective-permute-start(f32[768,3072]{1,0:T(8,128)} %get-tuple-element.192.refs_0_), channel_id=1, source_target_pairs={{0,1},{1,0},{2,3},{3,2},{4,5},{5,4},{6,7},{7,6}} | collective-permute-start | bytes 28311560 | tf_op jit(solution)/shard_map/ppermute | solution.py:457
  693.4 154.6 %collective-permute-start.37 = (f32[3072,768]{1,0:T(8,128)}, f32[3072,768]{1,0:T(8,128)}, u32[]{:S(2)}, u32[]{:S(2)}) collective-permute-start(f32[3072,768]{1,0:T(8,128)} %get-tuple-element.193.refs_1_), channel_id=1, source_target_pairs={{0,1},{1,0},{2,3},{3,2},{4,5},{5,4},{6,7},{7,6}} | collective-permute-start | bytes 28311560 | tf_op jit(solution)/shard_map/ppermute | solution.py:457
  693.4 131.6 %collective-permute-start.38 = (f32[768,768]{1,0:T(8,128)}, f32[768,768]{1,0:T(8,128)}, u32[]{:S(2)}, u32[]{:S(2)}) collective-permute-start(f32[768,768]{1,0:T(8,128)} %get-tuple-element.194.refs_2_), channel_id=1, source_target_pairs={{0,1},{1,0},{2,3},{3,2},{4,5},{5,4},{6,7},{7,6}} | collective-permute-start | bytes 7077896 | tf_op jit(solution)/shard_map/ppermute | solution.py:457
  824.9 176.8 %collective-permute-start.40 = (f32[4096,768]{1,0:T(8,128)}, f32[4096,768]{1,0:T(8,128)}, u32[]{:S(2)}, u32[]{:S(2)}) collective-permute-start(f32[4096,768]{1,0:T(8,128)} %get-tuple-element.253.refs_1_), channel_id=1, source_target_pairs={{0,1},{1,0},{2,3},{3,2},{4,5},{5,4},{6,7},{7,6}} | collective-permute-start | bytes 37748744 | tf_op jit(solution)/shard_map/ppermute | solution.py:458
  825.0 22.5 %collective-permute-start.39 = (f32[768,768]{1,0:T(8,128)}, f32[768,768]{1,0:T(8,128)S(1)}, u32[]{:S(2)}, u32[]{:S(2)}) collective-permute-start(f32[768,768]{1,0:T(8,128)} %get-tuple-element.195.refs_3_), channel_id=1, source_target_pairs={{0,1},{1,0},{2,3},{3,2},{4,5},{5,4},{6,7},{7,6}} | collective-permute-start | bytes 7077896 | tf_op jit(solution)/shard_map/ppermute | solution.py:457
  825.5 383.6 %all-gather.12.cloned.1.call-start = ((), (), s32[]{:S(2)}) async-start(), calls=%async_computation.1 | async-start | bytes 7864320 | tf_op jit(solution)/shard_map/all_gather | solution.py:394
  847.5 154.3 %collective-permute-start.41 = (f32[768,3072]{1,0:T(8,128)}, f32[768,3072]{1,0:T(8,128)}, u32[]{:S(2)}, u32[]{:S(2)}) collective-permute-start(f32[768,3072]{1,0:T(8,128)} %get-tuple-element.213.refs_0_), channel_id=1, source_target_pairs={{0,1},{1,0},{2,3},{3,2},{4,5},{5,4},{6,7},{7,6}} | collective-permute-start | bytes 28311560 | tf_op jit(solution)/shard_map/ppermute | solution.py:457
  847.6 154.1 %collective-permute-start.42 = (f32[3072,768]{1,0:T(8,128)}, f32[3072,768]{1,0:T(8,128)}, u32[]{:S(2)}, u32[]{:S(2)}) collective-permute-start(f32[3072,768]{1,0:T(8,128)} %get-tuple-element.214.refs_1_), channel_id=1, source_target_pairs={{0,1},{1,0},{2,3},{3,2},{4,5},{5,4},{6,7},{7,6}} | collective-permute-start | bytes 28311560 | tf_op jit(solution)/shard_map/ppermute | solution.py:457
  848.0 153.5 %collective-permute-start.43 = (f32[768,768]{1,0:T(8,128)}, f32[768,768]{1,0:T(8,128)}, u32[]{:S(2)}, u32[]{:S(2)}) collective-permute-start(f32[768,768]{1,0:T(8,128)} %get-tuple-element.215.refs_2_), channel_id=1, source_target_pairs={{0,1},{1,0},{2,3},{3,2},{4,5},{5,4},{6,7},{7,6}} | collective-permute-start | bytes 7077896 | tf_op jit(solution)/shard_map/ppermute | solution.py:457
  848.1 153.6 %collective-permute-start.44 = (f32[768,768]{1,0:T(8,128)}, f32[768,768]{1,0:T(8,128)}, u32[]{:S(2)}, u32[]{:S(2)}) collective-permute-start(f32[768,768]{1,0:T(8,128)} %get-tuple-element.216.refs_3_), channel_id=1, source_target_pairs={{0,1},{1,0},{2,3},{3,2},{4,5},{5,4},{6,7},{7,6}} | collective-permute-start | bytes 7077896 | tf_op jit(solution)/shard_map/ppermute | solution.py:457
  1001.5 183.9 %collective-permute-start.45 = (f32[4096,768]{1,0:T(8,128)}, f32[4096,768]{1,0:T(8,128)}, u32[]{:S(2)}, u32[]{:S(2)}) collective-permute-start(f32[4096,768]{1,0:T(8,128)} %get-tuple-element.254.refs_2_), channel_id=1, source_target_pairs={{0,1},{1,0},{2,3},{3,2},{4,5},{5,4},{6,7},{7,6}} | collective-permute-start | bytes 37748744 | tf_op jit(solution)/shard_map/ppermute | solution.py:458
  1028.0 157.1 %collective-permute-start.46 = (f32[768,3072]{1,0:T(8,128)}, f32[768,3072]{1,0:T(8,128)}, u32[]{:S(2)}, u32[]{:S(2)}) collective-permute-start(f32[768,3072]{1,0:T(8,128)} %get-tuple-element.233.refs_0_), channel_id=1, source_target_pairs={{0,1},{1,0},{2,3},{3,2},{4,5},{5,4},{6,7},{7,6}} | collective-permute-start | bytes 28311560 | tf_op jit(solution)/shard_map/ppermute | solution.py:457
  1028.4 157.1 %collective-permute-start.47 = (f32[3072,768]{1,0:T(8,128)}, f32[3072,768]{1,0:T(8,128)}, u32[]{:S(2)}, u32[]{:S(2)}) collective-permute-start(f32[3072,768]{1,0:T(8,128)} %get-tuple-element.234.refs_1_), channel_id=1, source_target_pairs={{0,1},{1,0},{2,3},{3,2},{4,5},{5,4},{6,7},{7,6}} | collective-permute-start | bytes 28311560 | tf_op jit(solution)/shard_map/ppermute | solution.py:457
  1028.5 156.1 %collective-permute-start.48 = (f32[768,768]{1,0:T(8,128)}, f32[768,768]{1,0:T(8,128)}, u32[]{:S(2)}, u32[]{:S(2)}) collective-permute-start(f32[768,768]{1,0:T(8,128)} %get-tuple-element.235.refs_2_), channel_id=1, source_target_pairs={{0,1},{1,0},{2,3},{3,2},{4,5},{5,4},{6,7},{7,6}} | collective-permute-start | bytes 7077896 | tf_op jit(solution)/shard_map/ppermute | solution.py:457
  1028.9 156.1 %collective-permute-start.49 = (f32[768,768]{1,0:T(8,128)}, f32[768,768]{1,0:T(8,128)}, u32[]{:S(2)}, u32[]{:S(2)}) collective-permute-start(f32[768,768]{1,0:T(8,128)} %get-tuple-element.236.refs_3_), channel_id=1, source_target_pairs={{0,1},{1,0},{2,3},{3,2},{4,5},{5,4},{6,7},{7,6}} | collective-permute-start | bytes 7077896 | tf_op jit(solution)/shard_map/ppermute | solution.py:457
  1184.6 189.6 %collective-permute-start.51 = (f32[4096,768]{1,0:T(8,128)}, f32[4096,768]{1,0:T(8,128)}, u32[]{:S(2)}, u32[]{:S(2)}) collective-permute-start(f32[4096,768]{1,0:T(8,128)} %get-tuple-element.255.refs_3_), channel_id=1, source_target_pairs={{0,1},{1,0},{2,3},{3,2},{4,5},{5,4},{6,7},{7,6}} | collective-permute-start | bytes 37748744 | tf_op jit(solution)/shard_map/ppermute | solution.py:458
  1185.0 188.7 %collective-permute-start.52 = (f32[768,3072]{1,0:T(8,128)}, f32[768,3072]{1,0:T(8,128)}, u32[]{:S(2)}, u32[]{:S(2)}) collective-permute-start(f32[768,3072]{1,0:T(8,128)} %get-tuple-element.259.refs_0_), channel_id=1, source_target_pairs={{0,1},{1,0},{2,3},{3,2},{4,5},{5,4},{6,7},{7,6}} | collective-permute-start | bytes 28311560 | tf_op jit(solution)/shard_map/ppermute | solution.py:457
  1185.1 151.5 %collective-permute-start.54 = (f32[768,768]{1,0:T(8,128)}, f32[768,768]{1,0:T(8,128)}, u32[]{:S(2)}, u32[]{:S(2)}) collective-permute-start(f32[768,768]{1,0:T(8,128)} %get-tuple-element.261.refs_2_), channel_id=1, source_target_pairs={{0,1},{1,0},{2,3},{3,2},{4,5},{5,4},{6,7},{7,6}} | collective-permute-start | bytes 7077896 | tf_op jit(solution)/shard_map/ppermute | solution.py:457
  1336.1 162.5 %collective-permute-start.50 = (f32[4096,768]{1,0:T(8,128)}, f32[4096,768]{1,0:T(8,128)}, u32[]{:S(2)}, u32[]{:S(2)}) collective-permute-start(f32[4096,768]{1,0:T(8,128)} %get-tuple-element.251.refs_0_), channel_id=1, source_target_pairs={{0,1},{1,0},{2,3},{3,2},{4,5},{5,4},{6,7},{7,6}} | collective-permute-start | bytes 37748744 | tf_op jit(solution)/shard_map/ppermute | solution.py:458
  1336.2 37.8 %collective-permute-start.53 = (f32[3072,768]{1,0:T(8,128)}, f32[3072,768]{1,0:T(8,128)}, u32[]{:S(2)}, u32[]{:S(2)}) collective-permute-start(f32[3072,768]{1,0:T(8,128)} %get-tuple-element.260.refs_1_), channel_id=1, source_target_pairs={{0,1},{1,0},{2,3},{3,2},{4,5},{5,4},{6,7},{7,6}} | collective-permute-start | bytes 28311560 | tf_op jit(solution)/shard_map/ppermute | solution.py:457
  1336.6 35.5 %collective-permute-start.55 = (f32[768,768]{1,0:T(8,128)}, f32[768,768]{1,0:T(8,128)S(1)}, u32[]{:S(2)}, u32[]{:S(2)}) collective-permute-start(f32[768,768]{1,0:T(8,128)} %get-tuple-element.262.refs_3_), channel_id=1, source_target_pairs={{0,1},{1,0},{2,3},{3,2},{4,5},{5,4},{6,7},{7,6}} | collective-permute-start | bytes 7077896 | tf_op jit(solution)/shard_map/ppermute | solution.py:457
  1373.5 98.8 %collective-permute-start.56 = (f32[768,3072]{1,0:T(8,128)}, f32[768,3072]{1,0:T(8,128)}, u32[]{:S(2)}, u32[]{:S(2)}) collective-permute-start(f32[768,3072]{1,0:T(8,128)} %get-tuple-element.264.refs_0_), channel_id=1, source_target_pairs={{0,1},{1,0},{2,3},{3,2},{4,5},{5,4},{6,7},{7,6}} | collective-permute-start | bytes 28311560 | tf_op jit(solution)/shard_map/ppermute | solution.py:457
  1373.7 98.7 %collective-permute-start.57 = (f32[3072,768]{1,0:T(8,128)}, f32[3072,768]{1,0:T(8,128)}, u32[]{:S(2)}, u32[]{:S(2)}) collective-permute-start(f32[3072,768]{1,0:T(8,128)} %get-tuple-element.265.refs_1_), channel_id=1, source_target_pairs={{0,1},{1,0},{2,3},{3,2},{4,5},{5,4},{6,7},{7,6}} | collective-permute-start | bytes 28311560 | tf_op jit(solution)/shard_map/ppermute | solution.py:457
  1374.0 98.3 %collective-permute-start.58 = (f32[768,768]{1,0:T(8,128)}, f32[768,768]{1,0:T(8,128)}, u32[]{:S(2)}, u32[]{:S(2)}) collective-permute-start(f32[768,768]{1,0:T(8,128)} %get-tuple-element.266.refs_2_), channel_id=1, source_target_pairs={{0,1},{1,0},{2,3},{3,2},{4,5},{5,4},{6,7},{7,6}} | collective-permute-start | bytes 7077896 | tf_op jit(solution)/shard_map/ppermute | solution.py:457
  1374.2 98.1 %collective-permute-start.59 = (f32[768,768]{1,0:T(8,128)}, f32[768,768]{1,0:T(8,128)}, u32[]{:S(2)}, u32[]{:S(2)}) collective-permute-start(f32[768,768]{1,0:T(8,128)} %get-tuple-element.267.refs_3_), channel_id=1, source_target_pairs={{0,1},{1,0},{2,3},{3,2},{4,5},{5,4},{6,7},{7,6}} | collective-permute-start | bytes 7077896 | tf_op jit(solution)/shard_map/ppermute | solution.py:457
  (40 other events, 553.0 us)
Sparse Core Ops, SparseCore 0:
  367.5 65.5 all-gather.31
  434.8 64.3 all-gather.27
  501.0 64.3 all-gather.29
  566.9 64.3 all-gather.25
  632.9 64.3 all-gather.23
  698.9 64.3 all-gather.21
  765.0 64.3 all-gather.19
  831.2 64.3 all-gather.17
  897.9 64.3 all-gather.15
  963.8 64.3 all-gather.13
  1030.0 64.3 all-gather.11
